TPU v7x, 128 devices: a whole 4x4x4 slice. The times are simulated.
128 devices in a mesh: dp: 32 (over x, z, y_hi), mp: 4 (over y_lo, core).
Axes of the slice: x: 4, y: 4 (y_hi: 2, y_lo: 2; y = y_hi * 2 + y_lo), z: 4, core: 2. Of those that a mesh axis runs over, the one named last changes fastest.
Arguments:
- initial_state: int32 [2048], P('dp'), may hold values from 0 to 255
- actions: int32 [2048, 16], P('dp'), may hold values from 0 to 15
- next_state: int32 [256, 16], replicated, may hold values from 0 to 255
- reward_table: float32 [256, 16], replicated, may hold values from -6 to 6
- reward_scale: float32 [2048], P('dp'), may hold values from 0.5 to 4.5
- observe_table: bfloat16 [256, 1024], replicated, may hold values from -6 to 6
- gain_attn: float32 [1024], replicated, may hold values from 0.5 to 1.5
- w_query: bfloat16 [1024, 1024], P(None, 'mp'), may hold values from -0.1875 to 0.1875
- w_key: bfloat16 [1024, 1024], P(None, 'mp'), may hold values from -0.1875 to 0.1875
- w_value: bfloat16 [1024, 1024], P(None, 'mp'), may hold values from -0.1875 to 0.1875
- w_out: bfloat16 [1024, 1024], P('mp'), may hold values from -0.1875 to 0.1875
- gain_mlp: float32 [1024], replicated, may hold values from 0.5 to 1.5
- w_up: bfloat16 [1024, 4096], P(None, 'mp'), may hold values from -0.1875 to 0.1875
- w_down: bfloat16 [4096, 1024], P('mp'), may hold values from -0.09375 to 0.09375
- gain_final: float32 [1024], replicated, may hold values from 0.5 to 1.5
- actor_head: bfloat16 [1024, 16], replicated, may hold values from -0.1875 to 0.1875
- critic_head: bfloat16 [1024], replicated, may hold values from -0.1875 to 0.1875
Outputs:
- grad_query: float32 [1024, 1024], P('dp', 'mp')
- grad_key: float32 [1024, 1024], P('dp', 'mp')
- grad_value: float32 [1024, 1024], P('dp', 'mp')
- grad_out: float32 [1024, 1024], P('mp', 'dp')
- grad_up: float32 [1024, 4096], P('dp', 'mp')
- grad_down: float32 [4096, 1024], P('mp', 'dp')
- grad_gain_attn: float32 [1024], P(('dp', 'mp'))
- grad_gain_mlp: float32 [1024], P('dp')
- grad_gain_final: float32 [1024], P('dp')
- grad_actor: float32 [1024, 16], P('dp')
- grad_critic: float32 [1024], P('dp')
All inputs are finite; a program needn't handle non-finite values.
Results may differ from a plain program's by a relative error of at most 0.015.
Values sent between devices are 32-bit elements; how exact they have to be, the bound alone decides.
A program may use at most 128 MiB of HBM per device.

v0:
```python
import functools
import math

import jax
import jax.numpy as jnp
from jax import lax
from jax.experimental import pallas as pl
from jax.experimental.pallas import tpu as pltpu
from jax.sharding import PartitionSpec as P

HEAD_DIM = 128
STEPS = 16
EPS = 1e-05
GAMMA = 0.9
VALUE_COEF = 0.5
ENTROPY_COEF = 0.1
MESH = pl.DeviceIdType.MESH
VMEM = pl.BlockSpec(memory_space=pltpu.VMEM)
F32 = jnp.float32
BF16 = jnp.bfloat16


def place():
    d, m = lax.axis_index("dp"), lax.axis_index("mp")
    return d, m, m % 2, m // 2


def partners():
    d, m, c, l = place()
    over = m + 2 - 4 * l
    return (d, m + 1 - 2 * c), (d, over), (d + 1 - 2 * (d % 2), over)


def greet(devices):
    barrier = pltpu.get_barrier_semaphore()
    for dev in devices:
        pl.semaphore_signal(barrier, inc=1, device_id=dev, device_id_type=MESH)
    pl.semaphore_wait(barrier, len(devices))


def remote(src, dst, send, recv, dev):
    return pltpu.make_async_remote_copy(
        src_ref=src, dst_ref=dst, send_sem=send, recv_sem=recv, device_id=dev, device_id_type=MESH
    )


def rows(start, size):
    return pl.ds(pl.multiple_of(start, size), size)


def by_blocks(total, block, body):
    lax.fori_loop(0, total // block, lambda i, z: (body(pl.multiple_of(i * block, block)), z)[1], 0)


def part_sums(p_ref, near, far, near_s, near_r, far_s, far_r, finish):
    d, m, c, l = place()
    core, *over = partners()
    step = 128
    first = []
    for k in range(2):
        blk = (1 - l) if k == 0 else l
        for h in range(2):
            cp = remote(
                p_ref.at[rows(h * 512 + (1 - c) * 256 + blk * step, step)],
                near.at[h, k], near_s.at[h, k], near_r.at[h, k], core,
            )
            cp.start()
            first.append(cp)

    def add_mine(h, k, blk):
        base = h * 512 + c * 256 + blk * step

        def body(i):
            near[h, k, pl.ds(i, 32), :] += p_ref[rows(base + i, 32), :]

        by_blocks(step, 32, body)

    second = []
    for h in range(2):
        first[h].wait_recv()
        add_mine(h, 0, 1 - l)
        cp = remote(near.at[h, 0], far.at[h], far_s.at[h], far_r.at[h], over[h])
        cp.start()
        second.append(cp)
    for h in range(2):
        first[2 + h].wait_recv()
        add_mine(h, 1, l)
    for h in range(2):
        second[h].wait_recv()
        finish(h)
    for cp in first + second:
        cp.wait_send()


def part_gather(q_ref, whole, out_ref, over_s, over_r, core_s, core_r, between=None):
    d, m, c, l = place()
    core, *over = partners()
    sent, incoming = [], []
    mine = [h * 512 + c * 256 + l * 128 for h in range(2)]
    yours = [h * 512 + c * 256 + (1 - l) * 128 for h in range(2)]
    for k in range(2):
        for h in range(2):
            cp = remote(
                q_ref.at[pl.ds(h * 128 + k * 64, 64)], whole.at[rows(mine[h] + k * 64, 64)],
                over_s.at[h, k], over_r.at[h, k], over[h],
            )
            cp.start()
            incoming.append((h, k, cp))
    for h in range(2):
        cp = remote(
            q_ref.at[pl.ds(h * 128, 128)], whole.at[rows(mine[h], 128)],
            core_s.at[h, 2], core_r.at[h, 2], core,
        )
        cp.start()
        sent.append(cp)

    def keep(base, size, src=None, at=0):
        def body(i):
            value = whole[rows(base + i, 32), :] if src is None else src[pl.ds(at + i, 32), :]
            out_ref[rows(base + i, 32), :] = value.astype(BF16)

        by_blocks(size, 32, body)

    for h in range(2):
        keep(mine[h], 128, q_ref, h * 128)
    for h in range(2):
        sent[h].wait_recv()
        keep(h * 512 + (1 - c) * 256 + l * 128, 128)
    if between is not None:
        between()
    for h, k, cp in incoming:
        cp.wait_recv()
        at = rows(yours[h] + k * 64, 64)
        fwd = remote(whole.at[at], whole.at[at], core_s.at[h, k], core_r.at[h, k], core)
        fwd.start()
        sent.append(fwd)
        keep(yours[h] + k * 64, 64)
    for n, (h, k, cp) in enumerate(incoming):
        sent[2 + n].wait_recv()
        keep(h * 512 + (1 - c) * 256 + (1 - l) * 128 + k * 64, 64)
    for cp in sent + [cp for _, _, cp in incoming]:
        cp.wait_send()


SUM_SCRATCH = [
    pltpu.VMEM((2, 2, 128, 1024), F32),
    pltpu.VMEM((2, 128, 1024), F32),
    pltpu.SemaphoreType.DMA((2, 2)),
    pltpu.SemaphoreType.DMA((2, 2)),
    pltpu.SemaphoreType.DMA((2,)),
    pltpu.SemaphoreType.DMA((2,)),
]
GATHER_SCRATCH = [
    pltpu.VMEM((1024, 1024), F32),
    pltpu.SemaphoreType.DMA((2, 2)),
    pltpu.SemaphoreType.DMA((2, 2)),
    pltpu.SemaphoreType.DMA((2, 3)),
    pltpu.SemaphoreType.DMA((2, 3)),
]


def params(n):
    return pltpu.CompilerParams(
        collective_id=n, has_side_effects=True, vmem_limit_bytes=60 * 1024 * 1024
    )


def attn_out_kernel(p_ref, xz_ref, gain_ref, x_ref, h_ref, near, far, *rest):
    sems, q_ref, gather = rest[:4], rest[4], rest[5:]
    greet(partners())

    def finish(h):
        def body(i):
            at = pl.ds(h * 128 + i, 32)
            x = near[h, 1, pl.ds(i, 32), :] + far[h, pl.ds(i, 32), :] + xz_ref[at, :]
            x_ref[at, :] = x
            inv = lax.rsqrt(jnp.mean(x * x, axis=-1, keepdims=True) + EPS)
            q_ref[at, :] = x * inv * gain_ref[...]

        by_blocks(128, 32, body)

    part_sums(p_ref, near, far, *sems, finish)
    part_gather(q_ref, gather[0], h_ref, *gather[1:])


def attn_out(partial, xz, gain):
    return pl.pallas_call(
        attn_out_kernel,
        out_shape=(jax.ShapeDtypeStruct((256, 1024), F32), jax.ShapeDtypeStruct((1024, 1024), BF16)),
        in_specs=[VMEM] * 3,
        out_specs=(VMEM, VMEM),
        scratch_shapes=[*SUM_SCRATCH, pltpu.VMEM((256, 1024), F32), *GATHER_SCRATCH],
        compiler_params=params(1),
        name="attn_out",
    )(partial, xz, gain.reshape(1, -1))


SCALE = 1.0 / math.sqrt(HEAD_DIM)


def dot(left, right, contract, **kw):
    return lax.dot_general(
        left, right, ((contract[:1], contract[1:]), ((), ())), preferred_element_type=F32, **kw
    )


def iota(shape, axis):
    return lax.broadcasted_iota(jnp.int32, shape, axis)


def block_probs(q, k):
    r, s = iota((128, 128), 0), iota((128, 128), 1)
    seen = ((r // STEPS) == (s // STEPS)) & (r >= s)
    weights = jnp.where(seen, jnp.exp(dot(q, k, (1, 1)) * SCALE), 0.0)
    return weights / jnp.sum(weights, axis=-1, keepdims=True)


def front_kernel(
    init_ref, act_ref, scale_ref, next_ref, rew_ref, obs_ref, gain_ref, wq_ref, wk_ref, wv_ref, wo_ref,
    p_ref, xz_ref, qkv_ref, match_ref, mixed_ref, ht_ref, own_ref,
    r_init, r_act, r_scale, tables, st_ref, sems,
):
    d, m, c, l = place()
    far = partners()[2]
    greet([far])
    copies = []
    for n, (src, dst) in enumerate(((init_ref, r_init), (act_ref, r_act), (scale_ref, r_scale))):
        cp = remote(src, dst, sems.at[0, n], sems.at[1, n], far)
        cp.start()
        copies.append(cp)

    def table_rows(i):
        at = pl.ds(i, 32)
        x = obs_ref[at, :].astype(F32)
        inv = lax.rsqrt(jnp.mean(x * x, axis=-1, keepdims=True) + EPS)
        ht_ref[at, :] = (x * inv * gain_ref[...]).astype(BF16)

    by_blocks(256, 32, table_rows)
    for n, w in enumerate((wq_ref, wk_ref, wv_ref)):
        tables[:, n * 256 : (n + 1) * 256] = dot(ht_ref[...], w[...], (1, 0)).astype(BF16)

    for cp in copies:
        cp.wait()
    swap = 32 + 64 * (1 - jnp.where(l == 0, 1, 0))
    lane = iota((1, 64), 1)
    state = jnp.where(lane >= swap, r_init[...], init_ref[...]).astype(F32)
    scale = jnp.where(lane >= swap, r_scale[...], scale_ref[...])
    act = jnp.where(iota((64, 16), 0) >= swap, r_act[...], act_ref[...]).astype(F32)
    eye = (iota((64, 64), 0) == iota((64, 64), 1)).astype(BF16)
    act_t = dot(act.astype(BF16), eye, (0, 0))
    nexts = next_ref[...].astype(F32).astype(BF16)
    ids, kinds = iota((256, 64), 0).astype(F32), iota((16, 64), 0).astype(F32)
    for t in range(STEPS):
        st_ref[pl.ds(t, 1), :] = state
        if t + 1 < STEPS:
            hit = jnp.where(ids == state, 1.0, 0.0).astype(BF16)
            found = dot(nexts, hit, (0, 0))
            state = jnp.sum(jnp.where(kinds == act_t[t : t + 1, :], found, 0.0), axis=0, keepdims=True)

    pick_t = (iota((128, 16), 0) % STEPS == iota((128, 16), 1)).astype(BF16)
    spread = jnp.ones((64, 128), BF16)
    lanes = iota((128, 128), 1).astype(F32)

    def per_token(rows_by_env, first_env):
        here = iota((128, 64), 1) == first_env + iota((128, 64), 0) // STEPS
        mixed = jnp.where(here, dot(pick_t, rows_by_env, (1, 0)), 0.0)
        return dot(mixed.astype(BF16), spread, (1, 0))

    def block(b, carry):
        at = rows(b * 128, 128)
        ids_here = per_token(st_ref[...].astype(BF16), b * 8)
        match = jnp.concatenate(
            [jnp.where(ids_here == lanes, 1.0, 0.0), jnp.where(ids_here == lanes + 128.0, 1.0, 0.0)], axis=1
        ).astype(BF16)
        match_ref[at, :] = match
        qkv = dot(match, tables[...], (1, 0)).astype(BF16)
        qkv_ref[at, :] = qkv
        heads = []
        for h in range(2):
            q, k, v = (qkv[:, n * 256 + h * 128 : n * 256 + (h + 1) * 128] for n in range(3))
            heads.append(dot(block_probs(q, k).astype(BF16), v, (1, 0)).astype(BF16))
        mixed = jnp.concatenate(heads, axis=1)
        mixed_ref[at, :] = mixed
        p_ref[at, :] = dot(mixed, wo_ref[...], (1, 0))
        return carry

    lax.fori_loop(0, 8, block, 0)

    for h in range(2):
        q = c * 2 + l
        at = pl.ds(h * 128, 128)
        mine = match_ref[rows(h * 512 + q * 128, 128), :]
        xz_ref[at, :] = dot(mine, obs_ref[...], (1, 0))
        first_env = h * 32 + q * 8
        acts = per_token(act_t.astype(BF16), first_env)
        chosen = jnp.where(acts == lanes, 1.0, 0.0)
        found = dot(mine.astype(F32), rew_ref[...], (1, 0), precision=lax.Precision.HIGHEST)
        here = iota((128, 64), 1) == first_env + iota((128, 64), 0) // STEPS
        factor = jnp.sum(jnp.where(here, scale, 0.0), axis=1, keepdims=True)
        reward = jnp.sum(chosen[:, :16] * found, axis=1, keepdims=True) * factor
        own_ref[at, :] = jnp.where(lanes == 16.0, reward, chosen)


def front(initial_state, actions, reward_scale, next_state, reward_table, observe_table, gain, wq, wk, wv, wo):
    sd = jax.ShapeDtypeStruct
    return pl.pallas_call(
        front_kernel,
        out_shape=(
            sd((1024, 1024), F32), sd((256, 1024), F32), sd((1024, 768), BF16), sd((1024, 256), BF16),
            sd((1024, 256), BF16), sd((256, 1024), BF16), sd((256, 128), F32),
        ),
        in_specs=[VMEM] * 11,
        out_specs=tuple([VMEM] * 7),
        scratch_shapes=[
            pltpu.VMEM((1, 64), jnp.int32), pltpu.VMEM((64, 16), jnp.int32), pltpu.VMEM((1, 64), F32),
            pltpu.VMEM((256, 768), BF16), pltpu.VMEM((16, 64), F32), pltpu.SemaphoreType.DMA((2, 3)),
        ],
        compiler_params=params(7),
        name="front",
    )(
        initial_state.reshape(1, -1), actions, reward_scale.reshape(1, -1), next_state, reward_table,
        observe_table, gain.reshape(1, -1), wq, wk, wv, wo,
    )


def axes_place():
    d, m, c, l = place()
    return d // 8, (d // 2) % 4, d % 2


def stats_devices():
    d, m, c, l = place()
    x, z, yh = axes_place()
    xdev = [(lax.rem(x + j, 4) * 8 + z * 2 + yh, m) for j in (1, 2, 3)]
    zdev = [(x * 8 + lax.rem(z + j, 4) * 2 + yh, m) for j in (1, 2, 3)]
    mine = yh * 4 + m
    ydev = []
    for j in range(1, 8):
        other = lax.rem(mine + j, 8)
        ydev.append((x * 8 + z * 2 + other // 4, other % 4))
    return xdev, zdev, ydev


def sum_everywhere(value, xs, zs, ys, xsem, zsem, ysem):
    d, m, c, l = place()
    x, z, yh = axes_place()
    xdev, zdev, ydev = stats_devices()

    def stage(slots, sems, devs, me, value):
        slots[me] = value
        copies = []
        for j, dev in enumerate(devs):
            cp = remote(slots.at[me], slots.at[me], sems.at[0, j], sems.at[1, j], dev)
            cp.start()
            copies.append(cp)
        for cp in copies:
            cp.wait_recv()
        total = slots[0]
        for k in range(1, len(devs) + 1):
            total = total + slots[k]
        for cp in copies:
            cp.wait_send()
        return total

    value = stage(xs, xsem, xdev, x, value)
    value = stage(zs, zsem, zdev, z, value)
    return stage(ys, ysem, ydev, yh * 4 + m, value)


STATS_SCRATCH = [
    pltpu.VMEM((4, 8, 128), F32),
    pltpu.VMEM((4, 8, 128), F32),
    pltpu.VMEM((8, 8, 128), F32),
    pltpu.SemaphoreType.DMA((2, 3)),
    pltpu.SemaphoreType.DMA((2, 3)),
    pltpu.SemaphoreType.DMA((2, 7)),
]


def fold8(term):
    total = term[0:8]
    for k in range(1, term.shape[0] // 8):
        total = total + term[8 * k : 8 * k + 8]
    return total


def loss_kernel(
    token_total, p_ref, x_ref, own_ref, heads_ref, gain_ref,
    dx_ref, low_ref, gh_ref, g_ref,
    near, far, s0, s1, s2, s3, xs, zs, ys, xsem, zsem, ysem, x2_ref, fin_ref, df_ref, *gather,
):
    xdev, zdev, ydev = stats_devices()
    greet(xdev + zdev + ydev)

    def finish(h):
        def body(i):
            at = pl.ds(h * 128 + i, 32)
            x = near[h, 1, pl.ds(i, 32), :] + far[h, pl.ds(i, 32), :] + x_ref[at, :]
            x2_ref[at, :] = x
            inv = lax.rsqrt(jnp.mean(x * x, axis=-1, keepdims=True) + EPS)
            fin_ref[at, :] = (x * inv * gain_ref[...]).astype(BF16)

        by_blocks(128, 32, body)

    part_sums(p_ref, near, far, s0, s1, s2, s3, finish)

    lane = iota((256, 128), 1)
    both = dot(fin_ref[...], heads_ref[...], (1, 0))
    critic = jnp.sum(jnp.where(lane == 16, both, 0.0), axis=1, keepdims=True)
    own = own_ref[...]
    reward = jnp.sum(jnp.where(lane == 16, own, 0.0), axis=1, keepdims=True)
    step = iota((256, 128), 0) % STEPS
    base = reward + jnp.where(step == STEPS - 1, GAMMA * critic, 0.0)
    r, s = iota((256, 256), 0), iota((256, 256), 1)
    ahead = ((r // STEPS) == (s // STEPS)) & (s >= r)
    decay = jnp.where(ahead, jnp.exp((s - r).astype(F32) * math.log(GAMMA)), 0.0)
    returns = dot(decay, base, (1, 0), precision=lax.Precision.HIGHEST)
    advantage = returns - critic
    sums = jnp.sum(advantage, axis=0, keepdims=True)
    squares = jnp.sum(advantage * advantage, axis=0, keepdims=True)
    tile = jnp.where(iota((8, 128), 0) == 0, sums, squares)
    totals = sum_everywhere(tile, xs, zs, ys, xsem, zsem, ysem)
    mean = totals[0:1, :] * (1.0 / token_total)
    spread = totals[1:2, :] * (1.0 / token_total) - mean * mean
    normed = (advantage - mean) * lax.rsqrt(spread + EPS)

    real = lane < 16
    logits = jnp.where(real, both, 0.0)
    mass = jnp.sum(jnp.where(real, jnp.exp(logits), 0.0), axis=1, keepdims=True)
    logp = jnp.where(real, logits - jnp.log(mass), 0.0)
    chance = jnp.where(real, jnp.exp(logp), 0.0)
    entropy = -jnp.sum(chance * logp, axis=1, keepdims=True)
    factor = 1.0 / math.sqrt(token_total)
    picked = jnp.where(real, own, 0.0)
    d_logits = factor * (-normed * (picked - chance) + ENTROPY_COEF * chance * (logp + entropy))
    d_value = (factor * VALUE_COEF) * (critic - returns)
    d_both = jnp.where(real, d_logits, jnp.where(lane == 16, d_value, 0.0)).astype(BF16)
    df_ref[...] = dot(d_both, heads_ref[...], (1, 1))

    g_ref[...] = jnp.zeros_like(g_ref)

    def back(i):
        at = pl.ds(i, 32)
        x, up = x2_ref[at, :], df_ref[at, :]
        inv = lax.rsqrt(jnp.mean(x * x, axis=-1, keepdims=True) + EPS)
        weighted = up * gain_ref[...]
        dx_ref[at, :] = inv * weighted - x * (inv * inv * inv) * jnp.mean(
            x * weighted, axis=-1, keepdims=True
        )
        g_ref[...] += fold8(up * x * inv)

    by_blocks(256, 32, back)
    part_gather(dx_ref, gather[0], low_ref, *gather[1:])
    gh_ref[...] = dot(fin_ref[...], d_both, (0, 0))


def loss(partial, x_one, own, heads, gain, token_total):
    sd = jax.ShapeDtypeStruct
    return pl.pallas_call(
        functools.partial(loss_kernel, token_total),
        out_shape=(sd((256, 1024), F32), sd((1024, 1024), BF16), sd((1024, 128), F32), sd((8, 1024), F32)),
        in_specs=[VMEM] * 5,
        out_specs=tuple([VMEM] * 4),
        scratch_shapes=[
            *SUM_SCRATCH, *STATS_SCRATCH, pltpu.VMEM((256, 1024), F32), pltpu.VMEM((256, 1024), BF16),
            pltpu.VMEM((256, 1024), F32), *GATHER_SCRATCH,
        ],
        compiler_params=params(2),
        name="loss",
    )(partial, x_one, own, heads, gain.reshape(1, -1))


class Ring:
    def __init__(self, src, bufs, sems, pos, right, left):
        self.src, self.pos, self.right, self.left = src, pos, right, left
        self.mid, self.fl, self.fr = bufs
        self.sems = sems
        self.copies = []

    def send(self, k, src, dst, dev):
        cp = remote(src, dst, self.sems.at[0, k], self.sems.at[1, k], dev)
        cp.start()
        self.copies.append(cp)

    def start(self):
        p = self.pos
        self.r, self.l, opp = lax.rem(p + 1, 4), lax.rem(p + 3, 4), lax.rem(p + 2, 4)
        self.send(0, self.src(opp, 0), self.mid.at[0], self.right)
        self.send(1, self.src(opp, 1), self.mid.at[1], self.left)
        self.send(2, self.src(self.r, 1), self.fl.at[1], self.right)
        self.send(3, self.src(self.l, 0), self.fr.at[0], self.left)

    def middle(self):
        self.copies[0].wait_recv()
        add_into(self.mid.at[0], self.src(self.r, 0))
        self.send(4, self.mid.at[0], self.fl.at[0], self.right)
        self.copies[1].wait_recv()
        add_into(self.mid.at[1], self.src(self.l, 1))
        self.send(5, self.mid.at[1], self.fr.at[1], self.left)

    def finish(self, out):
        for k in (2, 3, 4, 5):
            self.copies[k].wait_recv()
        for half in range(2):
            add_three(out(half), self.src(self.pos, half), self.fl.at[half], self.fr.at[half])

    def drain(self):
        for cp in self.copies:
            cp.wait_send()


def each_block(ref, body):
    if len(ref.shape) == 3:
        for k in range(ref.shape[0]):
            by_blocks(ref.shape[1], 8, lambda i, k=k: body((k, pl.ds(i, 8), slice(None))))
    else:
        by_blocks(ref.shape[0], 8, lambda i: body((pl.ds(i, 8), slice(None))))


def add_into(dst, src):
    def body(at):
        dst[at] += src[at]

    each_block(dst, body)


def add_three(dst, a, b, c):
    def body(at):
        dst[at] = a[at] + b[at] + c[at]

    each_block(dst, body)


def ring_one(order, src, bufs, sems):
    d, m, c, l = place()
    x, z, yh = axes_place()
    if order == "xz":
        return Ring(lambda j, h: src.at[j, pl.ds(h * 2, 2)], bufs, sems, x, at_x(1), at_x(3))
    return Ring(lambda j, h: src.at[pl.ds(h * 2, 2), j], bufs, sems, z, at_z(1), at_z(3))


def ring_two(order, res, bufs, sems):
    x, z, yh = axes_place()
    src = lambda j, h: res.at[j, pl.ds(h * 32, 32)]
    if order == "xz":
        return Ring(src, bufs, sems, z, at_z(1), at_z(3))
    return Ring(src, bufs, sems, x, at_x(1), at_x(3))


def at_x(k):
    d, m, c, l = place()
    x, z, yh = axes_place()
    return (lax.rem(x + k, 4) * 8 + z * 2 + yh, m)


def at_z(k):
    d, m, c, l = place()
    x, z, yh = axes_place()
    return (x * 8 + lax.rem(z + k, 4) * 2 + yh, m)


def one_scratch(w):
    return [pltpu.VMEM((2, 2, 64, w), F32)] * 3 + [pltpu.SemaphoreType.DMA((2, 6))]


def two_scratch(w):
    return [
        *[pltpu.VMEM((2, 32, w), F32)] * 3,
        pltpu.VMEM((64, w), F32),
        pltpu.VMEM((32, w), F32),
        pltpu.SemaphoreType.DMA((2, 6)),
        pltpu.SemaphoreType.DMA((2,)),
    ]


def mlp_in_back_kernel(
    p_ref, x_ref, dx_ref, gain_ref, up_ref, down_ref, o_ref, g_ref, up_res, down_res,
    near, far, s0, s1, s2, s3, q_ref, whole, g0, g1, g2, g3, um, ul, ur, us, dm, dl, dr, ds,
):
    greet([*partners(), at_x(1), at_x(3), at_z(1), at_z(3)])
    up_ring = ring_one("xz", up_ref, (um, ul, ur), us)
    down_ring = ring_one("zx", down_ref, (dm, dl, dr), ds)
    up_ring.start()
    down_ring.start()
    g_ref[...] = jnp.zeros_like(g_ref)

    def finish(h):
        def body(i):
            at = pl.ds(h * 128 + i, 32)
            up = near[h, 1, pl.ds(i, 32), :] + far[h, pl.ds(i, 32), :]
            x = x_ref[at, :]
            inv = lax.rsqrt(jnp.mean(x * x, axis=-1, keepdims=True) + EPS)
            weighted = up * gain_ref[...]
            back = inv * weighted - x * (inv * inv * inv) * jnp.mean(
                x * weighted, axis=-1, keepdims=True
            )
            q_ref[at, :] = dx_ref[at, :] + back
            g_ref[...] += fold8(up * x * inv)

        by_blocks(128, 32, body)

    part_sums(p_ref, near, far, s0, s1, s2, s3, finish)

    def between():
        up_ring.middle()
        down_ring.middle()

    part_gather(q_ref, whole, o_ref, g0, g1, g2, g3, between)
    up_ring.finish(lambda h: up_res.at[pl.ds(h * 2, 2)])
    down_ring.finish(lambda h: down_res.at[pl.ds(h * 2, 2)])
    up_ring.drain()
    down_ring.drain()


def mlp_in_back(partial, x_one, dx_two, gain, grad_up, grad_down):
    sd = jax.ShapeDtypeStruct
    return pl.pallas_call(
        mlp_in_back_kernel,
        out_shape=(
            sd((1024, 1024), BF16), sd((8, 1024), F32), sd((4, 64, 1024), F32), sd((4, 64, 1024), F32),
        ),
        in_specs=[VMEM] * 6,
        out_specs=tuple([VMEM] * 4),
        scratch_shapes=[
            *SUM_SCRATCH, pltpu.VMEM((256, 1024), F32), *GATHER_SCRATCH, *one_scratch(1024), *one_scratch(1024),
        ],
        compiler_params=params(4),
        name="mlp_in_back",
    )(
        partial, x_one, dx_two, gain.reshape(1, -1),
        grad_up.reshape(4, 4, 64, 1024), grad_down.reshape(4, 4, 64, 1024),
    )


def halves(value):
    high = value.astype(BF16)
    return high, (value - high.astype(F32)).astype(BF16)


def attend_back_kernel(
    dx_ref, wo_ref, qkv_ref, match_ref, ht_ref, obs_ref, wq_ref, wk_ref, wv_ref, gh_ref, gf_ref, gm_ref,
    qk_ref, v_ref, small_ref, sums, dt_ref, vec_ref,
):
    sums[...] = jnp.zeros_like(sums)

    def block(b, carry):
        at = rows(b * 128, 128)
        d_mixed = dot(dx_ref[at, :], wo_ref[...], (1, 1)).astype(BF16)
        qkv = qkv_ref[at, :]
        parts = [[], [], []]
        for h in range(2):
            q, k, v = (qkv[:, n * 256 + h * 128 : n * 256 + (h + 1) * 128] for n in range(3))
            up = d_mixed[:, h * 128 : (h + 1) * 128]
            probs = block_probs(q, k)
            d_probs = dot(up, v, (1, 1))
            parts[2].append(dot(probs.astype(BF16), up, (0, 0)).astype(BF16))
            d_scores = (
                probs * (d_probs - jnp.sum(probs * d_probs, axis=-1, keepdims=True)) * SCALE
            ).astype(BF16)
            parts[0].append(dot(d_scores, k, (1, 0)).astype(BF16))
            parts[1].append(dot(d_scores, q, (0, 0)).astype(BF16))
        d_qkv = jnp.concatenate([*parts[0], *parts[1], *parts[2]], axis=1)
        sums[...] += dot(match_ref[at, :], d_qkv, (0, 0))
        return carry

    lax.fori_loop(0, 8, block, 0)
    high, low = halves(sums[...])
    for i in range(4):
        cols = pl.ds(i * 256, 256)
        table = ht_ref[:, cols]
        total = dot(table, high, (0, 0)) + dot(table, low, (0, 0))
        qk_ref[cols, :] = total[:, :512]
        v_ref[cols, :] = total[:, 512:]
    dt_ref[...] = jnp.zeros_like(dt_ref)
    for n, w in enumerate((wq_ref, wk_ref, wv_ref)):
        cols = slice(n * 256, (n + 1) * 256)
        dt_ref[...] += dot(high[:, cols], w[...], (1, 1)) + dot(low[:, cols], w[...], (1, 1))
    vec_ref[0:8] = gf_ref[...]
    vec_ref[8:16] = gm_ref[...]
    vec_ref[16:32] = jnp.zeros((16, 1024), F32)

    def gain_rows(i):
        at = pl.ds(i, 32)
        x = obs_ref[at, :].astype(F32)
        inv = lax.rsqrt(jnp.mean(x * x, axis=-1, keepdims=True) + EPS)
        vec_ref[16:24] += fold8(dt_ref[at, :] * x * inv)

    by_blocks(256, 32, gain_rows)
    place_at = (iota((32, 128), 1) == 17 + iota((32, 128), 0) // 8).astype(BF16)
    vec = vec_ref[...]
    high, low = halves(vec)
    lowest = (vec - high.astype(F32) - low.astype(F32)).astype(BF16)
    small_ref[...] = gh_ref[...] + sum(dot(part, place_at, (0, 0)) for part in (high, low, lowest))


def attend_back(*args):
    sd = jax.ShapeDtypeStruct
    return pl.pallas_call(
        attend_back_kernel,
        out_shape=(sd((1024, 512), F32), sd((1024, 256), F32), sd((1024, 128), F32)),
        in_specs=[VMEM] * 12,
        out_specs=tuple([VMEM] * 3),
        scratch_shapes=[pltpu.VMEM((256, 768), F32), pltpu.VMEM((256, 1024), F32), pltpu.VMEM((32, 1024), F32)],
        compiler_params=pltpu.CompilerParams(vmem_limit_bytes=60 * 1024 * 1024),
        name="attend_back",
    )(*args)


FIRST = ("xz", "zx", "zx", "xz")
SECOND = ("xz", "zx") + FIRST


def grads_kernel(*refs):
    ins, outs, scratch = refs[:6], refs[6:12], refs[12:]
    mp_buf, mp_sem = scratch[-2:]
    d, m, c, l = place()
    x, z, yh = axes_place()
    yother = (d + 1 - 2 * yh, m)
    peers = [(d, lax.rem(m + j, 4)) for j in (1, 2, 3)]
    greet([at_x(1), at_x(3), at_z(1), at_z(3), yother] + peers)

    first, second, results = [], [], [ins[0], ins[1]]
    for i, order in enumerate(FIRST):
        mid, fl, fr, sems, res = scratch[5 * i : 5 * i + 5]
        first.append(ring_one(order, ins[2 + i], (mid, fl, fr), sems))
        results.append(res)
    at = 20
    ends = []
    for i, order in enumerate(SECOND):
        mid, fl, fr, res, ybuf, sems, ysem = scratch[at + 7 * i : at + 7 * i + 7]
        second.append(ring_two(order, results[i], (mid, fl, fr), sems))
        ends.append((res, ybuf, ysem))
    tails = []

    def send_tail(i):
        res, ybuf, ysem = ends[i]
        second[i].finish(lambda h: res.at[pl.ds(h * 32, 32)])
        cp = remote(res.at[rows((1 - yh) * 32, 32)], ybuf, ysem.at[0], ysem.at[1], yother)
        cp.start()
        tails.append(cp)

    for ring in first:
        ring.start()
    for ring in second[:2]:
        ring.start()
    for ring in first:
        ring.middle()
    for ring in second[:2]:
        ring.middle()
    for i, ring in enumerate(first):
        res = results[2 + i]
        ring.finish(lambda h, res=res: res.at[pl.ds(h * 2, 2)])
        second[2 + i].start()
    for i in range(2):
        send_tail(i)
    for ring in second[2:]:
        ring.middle()
    for i in (5, 2, 3, 4):
        send_tail(i)

    def total(i, put):
        res, ybuf, _ = ends[i]
        by_blocks(32, 8, lambda k: put(k, res[rows(yh * 32 + k, 8), :] + ybuf[pl.ds(k, 8), :]))

    def to_out(ref):
        def put(k, value):
            ref[pl.ds(k, 8), :] = value

        return put

    def to_mp(k, value):
        mp_buf[m, pl.ds(k, 8), :] = value

    shares = []
    for n, i in enumerate((0, 1, 5, 2, 3, 4)):
        tails[n].wait_recv()
        if i == 5:
            total(i, to_mp)
            for j, dev in enumerate(peers):
                cp = remote(mp_buf.at[m], mp_buf.at[m], mp_sem.at[0, j], mp_sem.at[1, j], dev)
                cp.start()
                shares.append(cp)
        else:
            total(i, to_out(outs[i]))
    for cp in shares:
        cp.wait_recv()
    outs[5][...] = mp_buf[0] + mp_buf[1] + mp_buf[2] + mp_buf[3]
    for cp in shares + tails:
        cp.wait_send()
    for ring in first + second:
        ring.drain()


def reduce_grads(up_res, down_res, qk, value, out, small):
    wide = [1024, 1024, 512, 256, 256, 128]
    scratch = []
    for w in wide[2:]:
        scratch += one_scratch(w) + [pltpu.VMEM((4, 64, w), F32)]
    for w in wide:
        scratch += two_scratch(w)
    scratch += [pltpu.VMEM((4, 32, 128), F32), pltpu.SemaphoreType.DMA((2, 3))]
    return pl.pallas_call(
        grads_kernel,
        out_shape=tuple(jax.ShapeDtypeStruct((32, w), F32) for w in wide),
        in_specs=[VMEM] * 6,
        out_specs=tuple([VMEM] * 6),
        scratch_shapes=scratch,
        compiler_params=params(6),
        name="reduce_grads",
    )(up_res, down_res, *[a.reshape(4, 4, 64, a.shape[1]) for a in (qk, value, out, small)])


def write_kernel(
    up_ref, down_ref, qk_ref, value_ref, out_ref, small_ref,
    o_q, o_k, o_v, o_out, o_up, o_down, o_attn, o_mlp, o_final, o_actor, o_critic,
):
    o_q[...] = qk_ref[:, :256]
    o_k[...] = qk_ref[:, 256:]
    o_v[...] = value_ref[...]
    o_up[...] = up_ref[...]
    o_out[...] = jnp.transpose(out_ref[...])
    o_down[...] = jnp.transpose(down_ref[...])
    o_actor[...] = small_ref[:, :16]
    flat = jnp.transpose(small_ref[...])
    o_critic[...] = flat[16:17, :]
    o_final[...] = flat[17:18, :]
    o_mlp[...] = flat[18:19, :]
    o_attn[...] = flat[19:20, :]


def write_outputs(*parts):
    sd = jax.ShapeDtypeStruct
    return pl.pallas_call(
        write_kernel,
        out_shape=(
            sd((32, 256), F32), sd((32, 256), F32), sd((32, 256), F32), sd((256, 32), F32), sd((32, 1024), F32),
            sd((1024, 32), F32), sd((1, 32), F32), sd((1, 32), F32), sd((1, 32), F32), sd((32, 16), F32),
            sd((1, 32), F32),
        ),
        in_specs=[VMEM] * 6,
        out_specs=tuple([VMEM] * 11),
        name="write_outputs",
    )(*parts)


def product(left, right):
    return jnp.dot(left, right, preferred_element_type=F32)


def across(left, right):
    return jnp.dot(left.T, right, preferred_element_type=F32)


def per_device(
    initial_state,
    actions,
    next_state,
    reward_table,
    reward_scale,
    observe_table,
    gain_attn,
    w_query,
    w_key,
    w_value,
    w_out,
    gain_mlp,
    w_up,
    w_down,
    gain_final,
    actor_head,
    critic_head,
):
    token_total = actions.size * lax.axis_size("dp")
    heads = jnp.concatenate(
        [actor_head, critic_head[:, None], jnp.zeros((actor_head.shape[0], 111), BF16)], axis=1
    )
    partial, own_zero, qkv, match, mixed, h_table, own = front(
        initial_state, actions, reward_scale, next_state, reward_table, observe_table, gain_attn,
        w_query, w_key, w_value, w_out,
    )
    x_one, h_two = attn_out(partial, own_zero, gain_mlp)
    up_rows = product(h_two, w_up)
    hidden = jax.nn.silu(up_rows).astype(BF16)
    dx_two, dx_two_low, grad_heads, final_terms = loss(
        product(hidden, w_down), x_one, own, heads, gain_final, token_total
    )
    grad_down = across(dx_two_low, hidden)
    d_hidden = jnp.dot(dx_two_low, w_down.T, preferred_element_type=F32).astype(BF16)
    sigmoid_up = jax.nn.sigmoid(up_rows)
    d_up = (
        d_hidden.astype(F32) * sigmoid_up * (1.0 + up_rows * (1.0 - sigmoid_up))
    ).astype(BF16)
    grad_up = across(h_two, d_up)
    dx_one_low, mlp_terms, up_res, down_res = mlp_in_back(
        product(d_up, w_up.T), x_one, dx_two, gain_mlp, grad_up, grad_down
    )
    grad_out = across(dx_one_low, mixed)
    grad_qk, grad_value, small = attend_back(
        dx_one_low, w_out, qkv, match, h_table, observe_table, w_query, w_key, w_value,
        grad_heads, final_terms, mlp_terms,
    )
    parts = reduce_grads(up_res, down_res, grad_qk, grad_value, grad_out, small)
    q, k, v, out, up, down, attn, mlp, final, actor, critic = write_outputs(*parts)
    attn_own = lax.dynamic_slice_in_dim(attn.reshape(-1), lax.axis_index("mp") * 8, 8, 0)
    return (
        q, k, v, out, up, down, attn_own, mlp.reshape(-1), final.reshape(-1), actor, critic.reshape(-1),
    )


def solution(mesh):
    return jax.shard_map(
        per_device,
        mesh=mesh,
        in_specs=(
            P("dp"),
            P("dp", None),
            P(),
            P(),
            P("dp"),
            P(),
            P(),
            P(None, "mp"),
            P(None, "mp"),
            P(None, "mp"),
            P("mp", None),
            P(),
            P(None, "mp"),
            P("mp", None),
            P(),
            P(),
            P(),
        ),
        out_specs=(
            P("dp", "mp"),
            P("dp", "mp"),
            P("dp", "mp"),
            P("mp", "dp"),
            P("dp", "mp"),
            P("mp", "dp"),
            P(("dp", "mp")),
            P("dp"),
            P("dp"),
            P("dp", None),
            P("dp"),
        ),
        check_vma=False,
    )
```

profile of v0, /device:TPU:0, one launch (start us, length us, event | category | flops | bytes accessed | tf_op | source)
XLA Modules:
  0.0 277.6 jit_solution(7392791292165741415)
XLA Ops:
  0.7 1.6 copy.36.next_ref
  2.3 1.5 copy.37.rew_ref
  3.8 1.4 copy.35.act_ref
  5.1 20.1 %front.1 = (f32[1024,1024]{1,0:T(8,128)}, f32[256,1024]{1,0:T(8,128)}, bf16[1024,768]{1,0:T(8,128)(2,1)}, bf16[1024,256]{1,0:T(8,128)(2,1)}, bf16[1024,256]{1,0:...) custom-call(s32[1,64]{1,0:T(1,128)} %bitcast.40, s32[64,16]{1,0:T(8,128)} %copy.35.act_ref, ...), custom_call_target="tpu_custom_call" | custom-call | tf_op jit(solution)/shard_map/front/pallas_call | solution.py:306
  25.3 37.0 %attn_out.1 = (f32[256,1024]{1,0:T(8,128)}, bf16[1024,1024]{1,0:T(8,128)(2,1)}) custom-call(f32[1024,1024]{1,0:T(8,128)} %get-tuple-element.48.p_ref, f32[256,1024]{1,0:T(8,128)} %get-tuple-element.49.xz_ref, f32[1,1024]{1,0:T(1,128)} %bitcast.36), custom_call_target="tpu_custom_call" | custom-call | tf_op jit(solution)/shard_map/attn_out/pallas_call | solution.py:187
  62.3 6.4 %multiply_convert_fusion.1 = (bf16[1024,1024]{1,0:T(8,128)(2,1)S(1)}, f32[1024,1024]{1,0:T(8,128)}) fusion(bf16[1024,1024]{1,0:T(8,128)(2,1)} %get-tuple-element.50, bf16[1024,1024]{1,0:T(8,128)(2,1)S(1)} %copy-done), kind=kOutput, calls=%fused_computation.1 | convolution fusion | flops 2152726528 | bytes 10485760 | tf_op jit(solution)/shard_map/dot_general | solution.py:847
  68.7 4.3 %fusion.p_ref = f32[1024,1024]{1,0:T(8,128)} fusion(bf16[1024,1024]{1,0:T(8,128)(2,1)S(1)} %get-tuple-element.107, bf16[1024,1024]{1,0:T(8,128)(2,1)S(1)} %copy-done.3), kind=kOutput, calls=%fused_computation.5 | convolution fusion | flops 2147483648 | bytes 8388608 | tf_op jit(solution)/shard_map/dot_general | solution.py:847
  73.0 0.2 broadcast_in_dim.8
  73.2 0.2 copy.38
  73.5 0.9 maximum_maximum_fusion.heads_ref
  74.3 55.5 %loss.1 = (f32[256,1024]{1,0:T(8,128)}, bf16[1024,1024]{1,0:T(8,128)(2,1)}, f32[1024,128]{1,0:T(8,128)}, f32[8,1024]{1,0:T(8,128)}) custom-call(f32[1024,1024]{1,0:T(8,128)} %fusion.p_ref, f32[256,1024]{1,0:T(8,128)} %get-tuple-element.51.x_ref, f32[256,128]{1,0:T(8,128)} %get-tuple-element.52.own_ref, bf16[1024,128]{1,0:T(8,128)(2,1)} %maximum_maximum_fusion.heads_ref, ...), custom_call_target="tpu_custom_call" | custom-call | tf_op jit(solution)/shard_map/loss/pallas_call | solution.py:459
  129.8 6.8 %multiply_convert_fusion = bf16[1024,1024]{1,0:T(8,128)(2,1)S(1)} fusion(f32[1024,1024]{1,0:T(8,128)} %get-tuple-element.108, bf16[1024,1024]{1,0:T(8,128)(2,1)} %get-tuple-element.53, bf16[1024,1024]{1,0:T(8,128)(2,1)} %param.30), kind=kOutput, calls=%fused_computation | convolution fusion | flops 2159017984 | bytes 10485760 | tf_op jit(solution)/shard_map/dot_general | solution.py:888
  136.6 4.4 %fusion.2 = f32[1024,1024]{1,0:T(8,128)} fusion(bf16[1024,1024]{1,0:T(8,128)(2,1)S(1)} %copy-done.4, bf16[1024,1024]{1,0:T(8,128)(2,1)S(1)} %multiply_convert_fusion), kind=kOutput, calls=%fused_computation.7 | convolution fusion | flops 2147483648 | bytes 8388608 | tf_op jit(solution)/shard_map/dot_general | solution.py:851
  141.0 4.4 %fusion.3 = f32[1024,1024]{1,0:T(8,128)} fusion(bf16[1024,1024]{1,0:T(8,128)(2,1)S(1)} %copy-done.5, bf16[1024,1024]{1,0:T(8,128)(2,1)S(1)} %copy-done.8), kind=kOutput, calls=%fused_computation.8 | convolution fusion | flops 2147483648 | bytes 8388608 | tf_op jit(solution)/shard_map/dot_general | solution.py:851
  145.4 4.3 %fusion.1.p_ref = f32[1024,1024]{1,0:T(8,128)} fusion(bf16[1024,1024]{1,0:T(8,128)(2,1)S(1)} %multiply_convert_fusion, bf16[1024,1024]{1,0:T(8,128)(2,1)S(1)} %copy-done), kind=kOutput, calls=%fused_computation.6 | convolution fusion | flops 2147483648 | bytes 8388608 | tf_op jit(solution)/shard_map/dot_general | solution.py:847
  149.8 46.6 %mlp_in_back.1 = (bf16[1024,1024]{1,0:T(8,128)(2,1)}, f32[8,1024]{1,0:T(8,128)}, f32[4,64,1024]{2,1,0:T(8,128)}, f32[4,64,1024]{2,1,0:T(8,128)}) custom-call(f32[1024,1024]{1,0:T(8,128)} %fusion.1.p_ref, f32[256,1024]{1,0:T(8,128)} %get-tuple-element.51.x_ref, f32[256,1024]{1,0:T(8,128)} %get-tuple-element.54.dx_ref, f32[1,1024]{1,0:T(1,128)} %bitcast.37, ...), custom_call_target="tpu_custom_call" | custom-call | tf_op jit(solution)/shard_map/mlp_in_back/pallas_call | solution.py:617
  196.4 3.3 %fusion.4 = f32[1024,256]{1,0:T(8,128)} fusion(bf16[1024,1024]{1,0:T(8,128)(2,1)} %get-tuple-element.57.dx_ref, bf16[1024,256]{1,0:T(8,128)(2,1)S(1)} %copy-done.6), kind=kOutput, calls=%fused_computation.9 | convolution fusion | flops 536870912 | bytes 3670016 | tf_op jit(solution)/shard_map/dot_general | solution.py:851
  199.7 19.1 %attend_back.1 = (f32[1024,512]{1,0:T(8,128)}, f32[1024,256]{1,0:T(8,128)}, f32[1024,128]{1,0:T(8,128)}) custom-call(bf16[1024,1024]{1,0:T(8,128)(2,1)} %get-tuple-element.57.dx_ref, bf16[256,1024]{1,0:T(8,128)(2,1)} %wo_ref.3, bf16[1024,768]{1,0:T(8,128)(2,1)} %get-tuple-element.58.qkv_ref, bf16[1024,256]{1,0:T(8,128)(2,1)} %get-tuple-element.59.match_ref, ...), custom_call_target="tpu_custom_call" | custom-call | tf_op jit(solution)/shard_map/attend_back/pallas_call | solution.py:698
  218.8 50.6 %reduce_grads.1 = (f32[32,1024]{1,0:T(8,128)}, f32[32,1024]{1,0:T(8,128)}, f32[32,512]{1,0:T(8,128)}, f32[32,256]{1,0:T(8,128)}, f32[32,256]{1,0:T(8,128)}, /*index=5*/f32[32,128]{1,0:T(8,128)}) custom-call(f32[4,64,1024]{2,1,0:T(8,128)} %get-tuple-element.55.refs_0_, f32[4,64,1024]{2,1,0:T(8,128)} %get-tuple-element.56.refs_1_, f32[4,4,64,512]{3,2,1,0:T(8,128)} %bitcast.32, ...), custom_call_target="tpu_custom_call" | custom-call | tf_op jit(solution)/shard_map/reduce_grads/pallas_call | solution.py:802
  269.4 2.1 write_outputs.1
  271.5 1.9 copy.41
  273.3 1.6 copy.40
  274.9 1.4 copy.42
  276.3 1.2 dynamic-slice_bitcast_fusion
  (20 shorter events, 0.1 us)
Async XLA Ops:
  0.6 61.6 %copy-start = (bf16[1024,1024]{1,0:T(8,128)(2,1)S(1)}, bf16[1024,1024]{1,0:T(8,128)(2,1)}, u32[]{:S(2)}) copy-start(bf16[1024,1024]{1,0:T(8,128)(2,1)} %param.29) | copy-start | bytes 6291460
  62.3 6.4 %copy-start.3 = (bf16[1024,1024]{1,0:T(8,128)(2,1)S(1)}, bf16[1024,1024]{1,0:T(8,128)(2,1)}, u32[]{:S(2)}) copy-start(bf16[1024,1024]{1,0:T(8,128)(2,1)} %param.30) | copy-start | bytes 6291460
  68.7 4.3 %copy-start.7 = (bf16[1024,1024]{1,0:T(8,128)(2,1)}, bf16[1024,1024]{1,0:T(8,128)(2,1)S(1)}, u32[]{:S(2)}) copy-start(bf16[1024,1024]{1,0:T(8,128)(2,1)S(1)} %get-tuple-element.107) | copy-start | bytes 6291460
  68.7 4.3 %copy-start.2 = (bf16[1024]{0:T(1024)(128)(2,1)S(1)}, bf16[1024]{0:T(1024)(128)(2,1)}, u32[]{:S(2)}) copy-start(bf16[1024]{0:T(1024)(128)(2,1)} %param.33) | copy-start | bytes 6148
  68.7 4.5 %copy-start.1 = (bf16[1024,16]{0,1:T(8,128)(2,1)S(1)}, bf16[1024,16]{0,1:T(8,128)(2,1)}, u32[]{:S(2)}) copy-start(bf16[1024,16]{0,1:T(8,128)(2,1)} %param.32) | copy-start | bytes 98308
  129.8 6.8 %copy-start.4 = (bf16[1024,1024]{1,0:T(8,128)(2,1)S(1)}, bf16[1024,1024]{1,0:T(8,128)(2,1)}, u32[]{:S(2)}) copy-start(bf16[1024,1024]{1,0:T(8,128)(2,1)} %get-tuple-element.50) | copy-start | bytes 6291460
  136.6 4.4 %copy-start.5 = (bf16[1024,1024]{1,0:T(8,128)(2,1)S(1)}, bf16[1024,1024]{1,0:T(8,128)(2,1)}, u32[]{:S(2)}) copy-start(bf16[1024,1024]{1,0:T(8,128)(2,1)} %get-tuple-element.53) | copy-start | bytes 6291460
  136.6 4.4 %copy-start.8 = (bf16[1024,1024]{1,0:T(8,128)(2,1)S(1)}, bf16[1024,1024]{1,0:T(8,128)(2,1)}, u32[]{:S(2)}) copy-start(bf16[1024,1024]{1,0:T(8,128)(2,1)} %copy-done.7) | copy-start | bytes 6291460
  149.8 46.6 %copy-start.6 = (bf16[1024,256]{1,0:T(8,128)(2,1)S(1)}, bf16[1024,256]{1,0:T(8,128)(2,1)}, u32[]{:S(2)}) copy-start(bf16[1024,256]{1,0:T(8,128)(2,1)} %get-tuple-element.66) | copy-start | bytes 1572868
where the time goes:
time: 279 us; the launch traced here: 278 us
  Pallas kernels  231 us (83%)
  matrix products  33.9 us (12%)
  local copies, waits for them, and re-layouts  11.1 us (4%)
    pallas_call x1, Pallas kernels, loss(): pl.pallas_call(functools.partial(loss_kernel, token_total), out_shape=(sd...  55.5 us
    pallas_call x1, Pallas kernels, reduce_grads(): pl.pallas_call(grads_kernel, out_shape=tuple((jax.ShapeDtypeStruct((32, w...  50.6 us
    pallas_call x1, Pallas kernels, mlp_in_back(): pl.pallas_call(mlp_in_back_kernel, out_shape=(sd((1024, 1024), BF16), sd(...  46.6 us
    pallas_call x1, Pallas kernels, attn_out(): pl.pallas_call(attn_out_kernel, out_shape=(jax.ShapeDtypeStruct((256, 102...  37 us
    pallas_call x1, Pallas kernels, front(): pl.pallas_call(front_kernel, out_shape=(sd((1024, 1024), F32), sd((256, 1...  20.1 us
    pallas_call x1, Pallas kernels, attend_back(): pl.pallas_call(attend_back_kernel, out_shape=(sd((1024, 512), F32), sd((1...  19.1 us
    dot_general x3, matrix products, product(): return jnp.dot(left, right, preferred_element_type=F32)  15 us
    dot_general x3, matrix products, across(): return jnp.dot(left.T, right, preferred_element_type=F32)  12.1 us

commit v1 on v0

v1 whole, which is shorter than its diff:
```python
import functools
import math

import jax
import jax.numpy as jnp
from jax import lax
from jax.experimental import pallas as pl
from jax.experimental.pallas import tpu as pltpu
from jax.sharding import PartitionSpec as P

HEAD_DIM = 128
STEPS = 16
EPS = 1e-05
GAMMA = 0.9
VALUE_COEF = 0.5
ENTROPY_COEF = 0.1
SCALE = 1.0 / math.sqrt(HEAD_DIM)
MESH = pl.DeviceIdType.MESH
VMEM = pl.BlockSpec(memory_space=pltpu.VMEM)
ANY = pl.BlockSpec(memory_space=pl.ANY)
F32 = jnp.float32
BF16 = jnp.bfloat16


def place():
    d, m = lax.axis_index("dp"), lax.axis_index("mp")
    return d, m, m % 2, m // 2


def axes_place():
    d, m, c, l = place()
    return d // 8, (d // 2) % 4, d % 2


def partners():
    d, m, c, l = place()
    over = m + 2 - 4 * l
    return (d, m + 1 - 2 * c), (d, over), (d + 1 - 2 * (d % 2), over)


def at_x(k):
    d, m, c, l = place()
    x, z, yh = axes_place()
    return (lax.rem(x + k, 4) * 8 + z * 2 + yh, m)


def at_z(k):
    d, m, c, l = place()
    x, z, yh = axes_place()
    return (x * 8 + lax.rem(z + k, 4) * 2 + yh, m)


def stats_devices():
    d, m, c, l = place()
    x, z, yh = axes_place()
    mine = yh * 4 + m
    ydev = []
    for j in range(1, 8):
        other = lax.rem(mine + j, 8)
        ydev.append((x * 8 + z * 2 + other // 4, other % 4))
    return [at_x(j) for j in (1, 2, 3)], [at_z(j) for j in (1, 2, 3)], ydev


def greet(devices):
    barrier = pltpu.get_barrier_semaphore()
    for dev in devices:
        pl.semaphore_signal(barrier, inc=1, device_id=dev, device_id_type=MESH)
    pl.semaphore_wait(barrier, len(devices))


def remote(src, dst, sems, at, dev):
    cp = pltpu.make_async_remote_copy(
        src_ref=src, dst_ref=dst, send_sem=sems.at[(0, *at)], recv_sem=sems.at[(1, *at)],
        device_id=dev, device_id_type=MESH,
    )
    cp.start()
    return cp


def rows(start, size):
    return pl.ds(pl.multiple_of(start, size), size)


def by_blocks(total, block, body):
    lax.fori_loop(0, total // block, lambda i, z: (body(pl.multiple_of(i * block, block)), z)[1], 0)


def dot(left, right, contract, **kw):
    return lax.dot_general(
        left, right, ((contract[:1], contract[1:]), ((), ())), preferred_element_type=F32, **kw
    )


def iota(shape, axis):
    return lax.broadcasted_iota(jnp.int32, shape, axis)


def fold8(term):
    total = term[0:8]
    for k in range(1, term.shape[0] // 8):
        total = total + term[8 * k : 8 * k + 8]
    return total


def inverse_rms(x):
    return lax.rsqrt(jnp.mean(x * x, axis=-1, keepdims=True) + EPS)


def norm_back(x, inv, gain, up):
    weighted = up * gain
    return inv * weighted - x * (inv * inv * inv) * jnp.mean(x * weighted, axis=-1, keepdims=True)


def block_at(h, core, low):
    return h * 512 + core * 256 + low * 128


CHUNKS = [(h, k) for k in range(2) for h in range(2)]


class Sums:
    def __init__(self, p, near_own, near_far, far, sems):
        d, m, self.c, self.l = place()
        self.core, *self.over = partners()
        self.p, self.near_own, self.near_far, self.far = p, near_own, near_far, far
        self.own_sem, self.near_sem, self.far_sem = sems
        self.own, self.near, self.sent = {}, {}, {}

    def give_own(self):
        for h in range(2):
            src = self.p.at[rows(block_at(h, 1 - self.c, self.l), 128)]
            self.own[h] = remote(src, self.near_own.at[h], self.own_sem, (h,), self.core)

    def give_far(self, k):
        for h in range(2):
            src = self.p.at[rows(block_at(h, 1 - self.c, 1 - self.l) + k * 64, 64)]
            self.near[h, k] = remote(src, self.near_far.at[h, k], self.near_sem, (h, k), self.core)

    def pass_far(self, k):
        for h in range(2):
            self.near[h, k].wait_recv()
            base = block_at(h, self.c, 1 - self.l) + k * 64

            def body(i, h=h, base=base):
                self.near_far[h, k, pl.ds(i, 32), :] += self.p[rows(base + i, 32), :]

            by_blocks(64, 32, body)
            self.sent[h, k] = remote(
                self.near_far.at[h, k], self.far.at[h, k], self.far_sem, (h, k), self.over[h]
            )

    def take_own(self):
        for h in range(2):
            self.own[h].wait_recv()

    def take(self, h, k):
        self.sent[h, k].wait_recv()

    def value(self, h, k, i):
        mine = self.p[rows(block_at(h, self.c, self.l) + k * 64 + i, 32), :]
        return mine + self.near_own[h, pl.ds(k * 64 + i, 32), :] + self.far[h, k, pl.ds(i, 32), :]

    def drain(self):
        for group in (self.own, self.near, self.sent):
            for cp in group.values():
                cp.wait_send()


class Gather:
    def __init__(self, q, whole, low, sems):
        d, m, self.c, self.l = place()
        self.core, *self.over = partners()
        self.q, self.whole, self.low = q, whole, low
        self.over_sem, self.core_sem, self.fwd_sem = sems
        self.far, self.near, self.fwd, self.left = {}, {}, {}, set()

    def keep(self, base, src=None, at=0):
        def body(i):
            value = self.whole[rows(base + i, 32), :] if src is None else src[pl.ds(at + i, 32), :]
            self.low[rows(base + i, 32), :] = value.astype(BF16)

        by_blocks(64, 32, body)

    def send(self, h, k):
        base = block_at(h, self.c, self.l) + k * 64
        src, dst = self.q.at[pl.ds(h * 128 + k * 64, 64)], self.whole.at[rows(base, 64)]
        self.far[h, k] = remote(src, dst, self.over_sem, (h, k), self.over[h])
        self.near[h, k] = remote(src, dst, self.core_sem, (h, k), self.core)
        self.keep(base, self.q, h * 128 + k * 64)

    def take_core(self, h, k):
        self.near[h, k].wait_recv()
        self.keep(block_at(h, 1 - self.c, self.l) + k * 64)

    def take_far(self, h, k):
        self.far[h, k].wait_recv()
        base = block_at(h, self.c, 1 - self.l) + k * 64
        at = self.whole.at[rows(base, 64)]
        self.fwd[h, k] = remote(at, at, self.fwd_sem, (h, k), self.core)
        self.keep(base)

    def forwarded(self, k):
        for h in range(2):
            self.fwd[h, k].wait_send()
        self.left.add(k)

    def take_fwd(self, h, k):
        self.fwd[h, k].wait_recv()
        self.keep(block_at(h, 1 - self.c, 1 - self.l) + k * 64)

    def drain(self):
        late = [cp for (h, k), cp in self.fwd.items() if k not in self.left]
        for cp in [*self.far.values(), *self.near.values(), *late]:
            cp.wait_send()


SUM_SEMS = [
    pltpu.SemaphoreType.DMA((2, 2)), pltpu.SemaphoreType.DMA((2, 2, 2)), pltpu.SemaphoreType.DMA((2, 2, 2)),
]
GATHER_SEMS = [pltpu.SemaphoreType.DMA((2, 2, 2))] * 3


def gather_work_sum(gather, sums, work):
    c, l = sums.c, sums.l
    work([(block_at(h, c, l), 128) for h in range(2)])
    for h, k in CHUNKS:
        gather.take_core(h, k)
    work([(block_at(h, 1 - c, l), 128) for h in range(2)])
    sums.give_own()
    for k in range(2):
        for h in range(2):
            gather.take_far(h, k)
        work([(block_at(h, c, 1 - l) + k * 64, 64) for h in range(2)])
        for h in range(2):
            gather.take_fwd(h, k)
        work([(block_at(h, 1 - c, 1 - l) + k * 64, 64) for h in range(2)])
        sums.give_far(k)
        gather.forwarded(k)
        sums.pass_far(k)
    sums.take_own()


def spans_of(ref, spans, cols=slice(None)):
    return jnp.concatenate([ref[rows(at, n), cols] for at, n in spans], axis=0)


def put_spans(ref, spans, cols, value):
    done = 0
    for at, n in spans:
        ref[rows(at, n), cols] = value[done : done + n]
        done += n


def sum_everywhere(value, xs, zs, ys, xsem, zsem, ysem):
    d, m, c, l = place()
    x, z, yh = axes_place()
    xdev, zdev, ydev = stats_devices()

    def stage(slots, sems, devs, me, value):
        slots[me] = value
        copies = [remote(slots.at[me], slots.at[me], sems, (j,), dev) for j, dev in enumerate(devs)]
        for cp in copies:
            cp.wait_recv()
        total = slots[0]
        for k in range(1, len(devs) + 1):
            total = total + slots[k]
        for cp in copies:
            cp.wait_send()
        return total

    value = stage(xs, xsem, xdev, x, value)
    value = stage(zs, zsem, zdev, z, value)
    return stage(ys, ysem, ydev, yh * 4 + m, value)


STATS_SCRATCH = [
    pltpu.VMEM((4, 8, 128), F32),
    pltpu.VMEM((4, 8, 128), F32),
    pltpu.VMEM((8, 8, 128), F32),
    pltpu.SemaphoreType.DMA((2, 3)),
    pltpu.SemaphoreType.DMA((2, 3)),
    pltpu.SemaphoreType.DMA((2, 7)),
]


class Ring:
    def __init__(self, src, bufs, sems, pos, right, left):
        self.src, self.pos, self.right, self.left = src, pos, right, left
        self.mid, self.fl, self.fr = bufs
        self.sems = sems
        self.copies = []

    def send(self, src, dst, dev):
        self.copies.append(remote(src, dst, self.sems, (len(self.copies),), dev))

    def start(self):
        p = self.pos
        self.r, self.l, opp = lax.rem(p + 1, 4), lax.rem(p + 3, 4), lax.rem(p + 2, 4)
        self.send(self.src(opp, 0), self.mid.at[0], self.right)
        self.send(self.src(opp, 1), self.mid.at[1], self.left)
        self.send(self.src(self.r, 1), self.fl.at[1], self.right)
        self.send(self.src(self.l, 0), self.fr.at[0], self.left)

    def middle(self):
        self.copies[0].wait_recv()
        add_into(self.mid.at[0], self.src(self.r, 0))
        self.send(self.mid.at[0], self.fl.at[0], self.right)
        self.copies[1].wait_recv()
        add_into(self.mid.at[1], self.src(self.l, 1))
        self.send(self.mid.at[1], self.fr.at[1], self.left)

    def finish(self, out):
        for k in (2, 3, 4, 5):
            self.copies[k].wait_recv()
        for half in range(2):
            add_three(out(half), self.src(self.pos, half), self.fl.at[half], self.fr.at[half])

    def drain(self):
        for cp in self.copies:
            cp.wait_send()


def each_block(ref, body):
    if len(ref.shape) == 3:
        for k in range(ref.shape[0]):
            by_blocks(ref.shape[1], 16, lambda i, k=k: body((k, pl.ds(i, 16), slice(None))))
    else:
        by_blocks(ref.shape[0], 16, lambda i: body((pl.ds(i, 16), slice(None))))


def add_into(dst, src):
    def body(at):
        dst[at] += src[at]

    each_block(dst, body)


def add_three(dst, a, b, c):
    def body(at):
        dst[at] = a[at] + b[at] + c[at]

    each_block(dst, body)


def ring_one(order, src, bufs, sems):
    x, z, yh = axes_place()
    if order == "xz":
        return Ring(lambda j, h: src.at[j, pl.ds(h * 2, 2)], bufs, sems, x, at_x(1), at_x(3))
    return Ring(lambda j, h: src.at[pl.ds(h * 2, 2), j], bufs, sems, z, at_z(1), at_z(3))


def ring_two(order, res, bufs, sems):
    x, z, yh = axes_place()

    def src(j, h):
        return res.at[j, pl.ds(h * 32, 32)]

    if order == "xz":
        return Ring(src, bufs, sems, z, at_z(1), at_z(3))
    return Ring(src, bufs, sems, x, at_x(1), at_x(3))


def one_scratch(w):
    return [pltpu.VMEM((2, 2, 64, w), F32)] * 3 + [pltpu.SemaphoreType.DMA((2, 6))]


def two_scratch(w):
    return [
        *[pltpu.VMEM((2, 32, w), F32)] * 3,
        pltpu.VMEM((64, w), F32),
        pltpu.VMEM((32, w), F32),
        pltpu.SemaphoreType.DMA((2, 6)),
        pltpu.SemaphoreType.DMA((2,)),
    ]


def params(n):
    return pltpu.CompilerParams(
        collective_id=n, has_side_effects=True, vmem_limit_bytes=63 * 1024 * 1024
    )


def block_probs(q, k):
    r, s = iota((128, 128), 0), iota((128, 128), 1)
    seen = ((r // STEPS) == (s // STEPS)) & (r >= s)
    weights = jnp.where(seen, jnp.exp(dot(q, k, (1, 1)) * SCALE), 0.0)
    return weights / jnp.sum(weights, axis=-1, keepdims=True)


def policy_kernel(
    token_total,
    init_ref, act_ref, scale_ref, next_ref, rew_ref, obs_ref, gain_attn, wq_ref, wk_ref, wv_ref, wo_ref,
    gain_mlp, gain_fin, actor_ref, critic_ref, up_hbm, down_hbm,
    qkv_ref, match_ref, mixed_ref, ht_ref, low_one, gh_ref, g_fin, g_mlp, up_res, down_res,
    r_init, r_act, r_scale, roll_sem, tables, st_ref, own_ref, head_f, heads,
    w_up, w_down, w_sem,
    p, near_own, near_far, far, whole, h_two, up_rows, hidden, low_two, d_up, x_one, dx_two, buf_a, buf_b,
    fin_ref, grad_up, grad_down, *rest,
):
    stats, rest = rest[:6], rest[6:]
    sems_a, sems_b, sems_d = rest[0:3], rest[3:6], rest[6:9]
    gs_b, gs_d, gs_e = rest[9:12], rest[12:15], rest[15:18]
    um, ul, ur, us, dm, dl, dr, ds = rest[18:26]
    d, m, c, l = place()
    weights = [
        pltpu.make_async_copy(up_hbm, w_up, w_sem.at[0]), pltpu.make_async_copy(down_hbm, w_down, w_sem.at[1]),
    ]
    for cp in weights:
        cp.start()
    xdev, zdev, ydev = stats_devices()
    greet(xdev + zdev + ydev)
    far_dev = partners()[2]
    copies = [
        remote(src, dst, roll_sem, (n,), far_dev)
        for n, (src, dst) in enumerate(((init_ref, r_init), (act_ref, r_act), (scale_ref, r_scale)))
    ]

    def table_rows(i):
        at = pl.ds(i, 32)
        x = obs_ref[at, :].astype(F32)
        ht_ref[at, :] = (x * inverse_rms(x) * gain_attn[...]).astype(BF16)

    by_blocks(256, 32, table_rows)
    for n, w in enumerate((wq_ref, wk_ref, wv_ref)):
        tables[:, n * 256 : (n + 1) * 256] = dot(ht_ref[...], w[...], (1, 0)).astype(BF16)
    head_f[...] = jnp.zeros_like(head_f)
    head_f[0:16, :] = actor_ref[...].astype(F32)
    head_f[16:17, :] = critic_ref[...].astype(F32)
    heads[...] = jnp.zeros_like(heads)
    heads[0:32, :] = head_f[...].astype(BF16)

    for cp in copies:
        cp.wait()
    swap = 32 + 64 * l
    lane = iota((1, 64), 1)
    state = jnp.where(lane >= swap, r_init[...], init_ref[...]).astype(F32)
    scale = jnp.where(lane >= swap, r_scale[...], scale_ref[...])
    act_t = jnp.where(iota((16, 64), 1) >= swap, r_act[...], act_ref[...]).astype(F32)
    nexts = next_ref[...].astype(F32).astype(BF16)
    ids, kinds = iota((256, 64), 0).astype(F32), iota((16, 64), 0).astype(F32)
    for t in range(STEPS):
        st_ref[pl.ds(t, 1), :] = state
        if t + 1 < STEPS:
            hit = jnp.where(ids == state, 1.0, 0.0).astype(BF16)
            found = dot(nexts, hit, (1, 0))
            state = jnp.sum(jnp.where(kinds == act_t[t : t + 1, :], found, 0.0), axis=0, keepdims=True)

    pick_t = (iota((128, 16), 0) % STEPS == iota((128, 16), 1)).astype(BF16)
    spread = jnp.ones((64, 128), BF16)
    lanes = iota((128, 128), 1).astype(F32)

    def per_token(rows_by_env, first_env):
        here = iota((128, 64), 1) == first_env + iota((128, 64), 0) // STEPS
        found = jnp.where(here, dot(pick_t, rows_by_env, (1, 0)), 0.0)
        return dot(found.astype(BF16), spread, (1, 0))

    def attend(core, low):
        def block(h, carry):
            at = rows(block_at(h, core, low), 128)
            ids_here = per_token(st_ref[...].astype(BF16), h * 32 + (core * 2 + low) * 8)
            match = jnp.concatenate(
                [jnp.where(ids_here == lanes, 1.0, 0.0), jnp.where(ids_here == lanes + 128.0, 1.0, 0.0)], axis=1
            ).astype(BF16)
            match_ref[at, :] = match
            qkv = dot(match, tables[...], (1, 0)).astype(BF16)
            qkv_ref[at, :] = qkv
            outs = []
            for n in range(2):
                q, k, v = (qkv[:, j * 256 + n * 128 : j * 256 + (n + 1) * 128] for j in range(3))
                outs.append(dot(block_probs(q, k).astype(BF16), v, (1, 0)).astype(BF16))
            mixed = jnp.concatenate(outs, axis=1)
            mixed_ref[at, :] = mixed
            p[at, :] = dot(mixed, wo_ref[...], (1, 0))
            return carry

        lax.fori_loop(0, 2, block, 0)

    sums = Sums(p, near_own, near_far, far, sems_a)
    attend(1 - c, 1 - l)
    sums.give_far(0)
    sums.give_far(1)
    attend(c, 1 - l)
    sums.pass_far(0)
    sums.pass_far(1)
    attend(1 - c, l)
    sums.give_own()
    attend(c, l)
    for h in range(2):
        at = pl.ds(h * 128, 128)
        mine = match_ref[rows(block_at(h, c, l), 128), :]
        x_one[at, :] = dot(mine, obs_ref[...], (1, 0))
        first_env = h * 32 + (c * 2 + l) * 8
        chosen = jnp.where(per_token(act_t.astype(BF16), first_env) == lanes, 1.0, 0.0)
        found = dot(mine.astype(F32), rew_ref[...], (1, 1), precision=lax.Precision.HIGHEST)
        here = iota((128, 64), 1) == first_env + iota((128, 64), 0) // STEPS
        factor = jnp.sum(jnp.where(here, scale, 0.0), axis=1, keepdims=True)
        reward = jnp.sum(chosen[:, :16] * found, axis=1, keepdims=True) * factor
        own_ref[at, :] = jnp.where(lanes == 16.0, reward, chosen)
    sums.take_own()

    gather = Gather(buf_a, whole, h_two, gs_b)
    for h, k in CHUNKS:
        sums.take(h, k)

        def body(i, h=h, k=k):
            at = pl.ds(h * 128 + k * 64 + i, 32)
            x = sums.value(h, k, i) + x_one[at, :]
            x_one[at, :] = x
            buf_a[at, :] = x * inverse_rms(x) * gain_mlp[...]

        by_blocks(64, 32, body)
        gather.send(h, k)
    sums.drain()
    for cp in weights:
        cp.wait()

    def forward(spans):
        def up(j):
            cols = pl.ds(j, 256)
            u = dot(spans_of(h_two, spans), w_up[:, cols], (1, 0))
            put_spans(up_rows, spans, cols, u)
            put_spans(hidden, spans, cols, (u / (1.0 + jnp.exp(-u))).astype(BF16))

        def down(j):
            cols = pl.ds(j, 256)
            put_spans(p, spans, cols, dot(spans_of(hidden, spans), w_down[:, cols], (1, 0)))

        by_blocks(1024, 256, up)
        by_blocks(1024, 256, down)

    sums = Sums(p, near_own, near_far, far, sems_b)
    gather_work_sum(gather, sums, forward)
    for h, k in CHUNKS:
        sums.take(h, k)

        def body(i, h=h, k=k):
            at = pl.ds(h * 128 + k * 64 + i, 32)
            x = sums.value(h, k, i) + x_one[at, :]
            buf_b[at, :] = x
            fin_ref[at, :] = (x * inverse_rms(x) * gain_fin[...]).astype(BF16)

        by_blocks(64, 32, body)
    gather.drain()
    sums.drain()

    lane = iota((256, 128), 1)
    both = dot(fin_ref[...], heads[...], (1, 1))
    critic = jnp.sum(jnp.where(lane == 16, both, 0.0), axis=1, keepdims=True)
    own = own_ref[...]
    reward = jnp.sum(jnp.where(lane == 16, own, 0.0), axis=1, keepdims=True)
    step = iota((256, 128), 0) % STEPS
    base = reward + jnp.where(step == STEPS - 1, GAMMA * critic, 0.0)
    r, s = iota((256, 256), 0), iota((256, 256), 1)
    ahead = ((r // STEPS) == (s // STEPS)) & (s >= r)
    decay = jnp.where(ahead, jnp.exp((s - r).astype(F32) * math.log(GAMMA)), 0.0)
    returns = dot(decay, base, (1, 0), precision=lax.Precision.HIGHEST)
    advantage = returns - critic
    tile = jnp.where(
        iota((8, 128), 0) == 0,
        jnp.sum(advantage, axis=0, keepdims=True),
        jnp.sum(advantage * advantage, axis=0, keepdims=True),
    )
    totals = sum_everywhere(tile, *stats)
    mean = totals[0:1, :] * (1.0 / token_total)
    variance = totals[1:2, :] * (1.0 / token_total) - mean * mean
    normed = (advantage - mean) * lax.rsqrt(variance + EPS)
    real = lane < 16
    logits = jnp.where(real, both, 0.0)
    mass = jnp.sum(jnp.where(real, jnp.exp(logits), 0.0), axis=1, keepdims=True)
    logp = jnp.where(real, logits - jnp.log(mass), 0.0)
    chance = jnp.where(real, jnp.exp(logp), 0.0)
    entropy = -jnp.sum(chance * logp, axis=1, keepdims=True)
    factor = 1.0 / math.sqrt(token_total)
    picked = jnp.where(real, own, 0.0)
    d_logits = factor * (-normed * (picked - chance) + ENTROPY_COEF * chance * (logp + entropy))
    d_value = (factor * VALUE_COEF) * (critic - returns)
    d_both = jnp.where(real, d_logits, jnp.where(lane == 16, d_value, 0.0)).astype(BF16)
    buf_a[...] = dot(d_both, heads[...], (1, 0))
    g_fin[...] = jnp.zeros_like(g_fin)
    g_mlp[...] = jnp.zeros_like(g_mlp)

    gather = Gather(dx_two, whole, low_two, gs_d)
    for h, k in CHUNKS:

        def body(i, h=h, k=k):
            at = pl.ds(h * 128 + k * 64 + i, 32)
            x, up = buf_b[at, :], buf_a[at, :]
            inv = inverse_rms(x)
            dx_two[at, :] = norm_back(x, inv, gain_fin[...], up)
            g_fin[...] += fold8(up * x * inv)

        by_blocks(64, 32, body)
        gather.send(h, k)
    gh_ref[...] = dot(fin_ref[...], d_both, (0, 0))

    def backward(spans):
        def up(j):
            cols = pl.ds(j, 256)
            d_hidden = dot(spans_of(low_two, spans), w_down[cols, :], (1, 1)).astype(BF16).astype(F32)
            u = spans_of(up_rows, spans, cols)
            sig = 1.0 / (1.0 + jnp.exp(-u))
            put_spans(d_up, spans, cols, (d_hidden * sig * (1.0 + u * (1.0 - sig))).astype(BF16))

        def down(j):
            cols = pl.ds(j, 256)
            put_spans(p, spans, cols, dot(spans_of(d_up, spans), w_up[cols, :], (1, 1)))

        by_blocks(1024, 256, up)
        by_blocks(1024, 256, down)

    sums = Sums(p, near_own, near_far, far, sems_d)
    gather_work_sum(gather, sums, backward)

    def weight_grad(out, left, right):
        def tile(j, carry):
            cols = rows(j * 256, 256)
            out[j] = dot(left[:, cols], right[...], (0, 0)).reshape(4, 64, 1024)
            return carry

        lax.fori_loop(0, 4, tile, 0)

    up_ring = ring_one("xz", grad_up, (um, ul, ur), us)
    down_ring = ring_one("zx", grad_down, (dm, dl, dr), ds)
    weight_grad(grad_up, h_two, d_up)
    up_ring.start()
    weight_grad(grad_down, low_two, hidden)
    down_ring.start()
    gather.drain()

    gather = Gather(buf_b, whole, low_one, gs_e)
    for h, k in CHUNKS:
        sums.take(h, k)

        def body(i, h=h, k=k):
            at = pl.ds(h * 128 + k * 64 + i, 32)
            up, x = sums.value(h, k, i), x_one[at, :]
            inv = inverse_rms(x)
            buf_b[at, :] = dx_two[at, :] + norm_back(x, inv, gain_mlp[...], up)
            g_mlp[...] += fold8(up * x * inv)

        by_blocks(64, 32, body)
        gather.send(h, k)
    sums.drain()
    for h, k in CHUNKS:
        gather.take_core(h, k)
    for h in range(2):
        gather.take_far(h, 0)
    up_ring.middle()
    down_ring.middle()
    for h in range(2):
        gather.take_far(h, 1)
    for h, k in CHUNKS:
        gather.take_fwd(h, k)
    gather.drain()
    up_ring.finish(lambda h: up_res.at[pl.ds(h * 2, 2)])
    down_ring.finish(lambda h: down_res.at[pl.ds(h * 2, 2)])
    up_ring.drain()
    down_ring.drain()


def policy(token_total, *args):
    sd, vm = jax.ShapeDtypeStruct, pltpu.VMEM
    return pl.pallas_call(
        functools.partial(policy_kernel, token_total),
        out_shape=(
            sd((1024, 768), BF16), sd((1024, 256), BF16), sd((1024, 256), BF16), sd((256, 1024), BF16),
            sd((1024, 1024), BF16), sd((1024, 128), F32), sd((8, 1024), F32), sd((8, 1024), F32),
            sd((4, 64, 1024), F32), sd((4, 64, 1024), F32),
        ),
        in_specs=[VMEM] * 15 + [ANY] * 2,
        out_specs=tuple([VMEM] * 10),
        scratch_shapes=[
            vm((1, 64), jnp.int32), vm((16, 64), jnp.int32), vm((1, 64), F32), pltpu.SemaphoreType.DMA((2, 3)),
            vm((256, 768), BF16), vm((16, 64), F32), vm((256, 128), F32), vm((32, 1024), F32), vm((128, 1024), BF16),
            vm((1024, 1024), BF16), vm((1024, 1024), BF16), pltpu.SemaphoreType.DMA((2,)),
            vm((1024, 1024), F32), vm((2, 128, 1024), F32), vm((2, 2, 64, 1024), F32), vm((2, 2, 64, 1024), F32),
            vm((1024, 1024), F32), vm((1024, 1024), BF16), vm((1024, 1024), F32), vm((1024, 1024), BF16),
            vm((1024, 1024), BF16), vm((1024, 1024), BF16),
            vm((256, 1024), F32), vm((256, 1024), F32), vm((256, 1024), F32), vm((256, 1024), F32),
            vm((256, 1024), BF16), vm((4, 4, 64, 1024), F32), vm((4, 4, 64, 1024), F32),
            *STATS_SCRATCH, *SUM_SEMS, *SUM_SEMS, *SUM_SEMS, *GATHER_SEMS, *GATHER_SEMS, *GATHER_SEMS,
            *one_scratch(1024), *one_scratch(1024),
        ],
        compiler_params=params(1),
        name="policy",
    )(*args)


def halves(value):
    high = value.astype(BF16)
    return high, (value - high.astype(F32)).astype(BF16)


def attend_back_kernel(
    dx_ref, wo_ref, qkv_ref, match_ref, ht_ref, obs_ref, wq_ref, wk_ref, wv_ref, gh_ref, gf_ref, gm_ref,
    qk_ref, v_ref, small_ref, sums, dt_ref, vec_ref,
):
    sums[...] = jnp.zeros_like(sums)

    def block(b, carry):
        at = rows(b * 128, 128)
        d_mixed = dot(dx_ref[at, :], wo_ref[...], (1, 1)).astype(BF16)
        qkv = qkv_ref[at, :]
        parts = [[], [], []]
        for h in range(2):
            q, k, v = (qkv[:, n * 256 + h * 128 : n * 256 + (h + 1) * 128] for n in range(3))
            up = d_mixed[:, h * 128 : (h + 1) * 128]
            probs = block_probs(q, k)
            d_probs = dot(up, v, (1, 1))
            parts[2].append(dot(probs.astype(BF16), up, (0, 0)).astype(BF16))
            d_scores = (
                probs * (d_probs - jnp.sum(probs * d_probs, axis=-1, keepdims=True)) * SCALE
            ).astype(BF16)
            parts[0].append(dot(d_scores, k, (1, 0)).astype(BF16))
            parts[1].append(dot(d_scores, q, (0, 0)).astype(BF16))
        d_qkv = jnp.concatenate([*parts[0], *parts[1], *parts[2]], axis=1)
        sums[...] += dot(match_ref[at, :], d_qkv, (0, 0))
        return carry

    lax.fori_loop(0, 8, block, 0)
    high, low = halves(sums[...])
    for i in range(4):
        cols = pl.ds(i * 256, 256)
        table = ht_ref[:, cols]
        total = dot(table, high, (0, 0)) + dot(table, low, (0, 0))
        qk_ref[cols, :] = total[:, :512]
        v_ref[cols, :] = total[:, 512:]
    dt_ref[...] = jnp.zeros_like(dt_ref)
    for n, w in enumerate((wq_ref, wk_ref, wv_ref)):
        cols = slice(n * 256, (n + 1) * 256)
        dt_ref[...] += dot(high[:, cols], w[...], (1, 1)) + dot(low[:, cols], w[...], (1, 1))
    vec_ref[0:8] = gf_ref[...]
    vec_ref[8:16] = gm_ref[...]
    vec_ref[16:32] = jnp.zeros((16, 1024), F32)

    def gain_rows(i):
        at = pl.ds(i, 32)
        x = obs_ref[at, :].astype(F32)
        inv = lax.rsqrt(jnp.mean(x * x, axis=-1, keepdims=True) + EPS)
        vec_ref[16:24] += fold8(dt_ref[at, :] * x * inv)

    by_blocks(256, 32, gain_rows)
    place_at = (iota((32, 128), 1) == 17 + iota((32, 128), 0) // 8).astype(BF16)
    vec = vec_ref[...]
    high, low = halves(vec)
    lowest = (vec - high.astype(F32) - low.astype(F32)).astype(BF16)
    small_ref[...] = gh_ref[...] + sum(dot(part, place_at, (0, 0)) for part in (high, low, lowest))


def attend_back(*args):
    sd = jax.ShapeDtypeStruct
    return pl.pallas_call(
        attend_back_kernel,
        out_shape=(sd((1024, 512), F32), sd((1024, 256), F32), sd((1024, 128), F32)),
        in_specs=[VMEM] * 12,
        out_specs=tuple([VMEM] * 3),
        scratch_shapes=[pltpu.VMEM((256, 768), F32), pltpu.VMEM((256, 1024), F32), pltpu.VMEM((32, 1024), F32)],
        compiler_params=pltpu.CompilerParams(vmem_limit_bytes=40 * 1024 * 1024),
        name="attend_back",
    )(*args)


FIRST = ("xz", "zx", "zx", "xz")
SECOND = ("xz", "zx") + FIRST


def grads_kernel(*refs):
    ins, outs, scratch = refs[:6], refs[6:12], refs[12:]
    mp_buf, mp_sem = scratch[-2:]
    d, m, c, l = place()
    x, z, yh = axes_place()
    yother = (d + 1 - 2 * yh, m)
    peers = [(d, lax.rem(m + j, 4)) for j in (1, 2, 3)]
    greet([at_x(1), at_x(3), at_z(1), at_z(3), yother] + peers)

    first, second, results = [], [], [ins[0], ins[1]]
    for i, order in enumerate(FIRST):
        mid, fl, fr, sems, res = scratch[5 * i : 5 * i + 5]
        first.append(ring_one(order, ins[2 + i], (mid, fl, fr), sems))
        results.append(res)
    at = 20
    ends = []
    for i, order in enumerate(SECOND):
        mid, fl, fr, res, ybuf, sems, ysem = scratch[at + 7 * i : at + 7 * i + 7]
        second.append(ring_two(order, results[i], (mid, fl, fr), sems))
        ends.append((res, ybuf, ysem))
    tails = []

    def send_tail(i):
        res, ybuf, ysem = ends[i]
        second[i].finish(lambda h: res.at[pl.ds(h * 32, 32)])
        tails.append(remote(res.at[rows((1 - yh) * 32, 32)], ybuf, ysem, (), yother))

    for ring in first:
        ring.start()
    for ring in second[:2]:
        ring.start()
    for ring in first:
        ring.middle()
    for ring in second[:2]:
        ring.middle()
    for i, ring in enumerate(first):
        res = results[2 + i]
        ring.finish(lambda h, res=res: res.at[pl.ds(h * 2, 2)])
        second[2 + i].start()
    for i in range(2):
        send_tail(i)
    for ring in second[2:]:
        ring.middle()
    for i in (5, 2, 3, 4):
        send_tail(i)

    def total(i, put):
        res, ybuf, _ = ends[i]
        by_blocks(32, 8, lambda k: put(k, res[rows(yh * 32 + k, 8), :] + ybuf[pl.ds(k, 8), :]))

    def to_out(ref):
        def put(k, value):
            ref[pl.ds(k, 8), :] = value

        return put

    def to_mp(k, value):
        mp_buf[m, pl.ds(k, 8), :] = value

    shares = []
    for n, i in enumerate((0, 1, 5, 2, 3, 4)):
        tails[n].wait_recv()
        if i == 5:
            total(i, to_mp)
            for j, dev in enumerate(peers):
                shares.append(remote(mp_buf.at[m], mp_buf.at[m], mp_sem, (j,), dev))
        else:
            total(i, to_out(outs[i]))
    for cp in shares:
        cp.wait_recv()
    outs[5][...] = mp_buf[0] + mp_buf[1] + mp_buf[2] + mp_buf[3]
    for cp in shares + tails:
        cp.wait_send()
    for ring in first + second:
        ring.drain()


def reduce_grads(up_res, down_res, qk, value, out, small):
    wide = [1024, 1024, 512, 256, 256, 128]
    scratch = []
    for w in wide[2:]:
        scratch += one_scratch(w) + [pltpu.VMEM((4, 64, w), F32)]
    for w in wide:
        scratch += two_scratch(w)
    scratch += [pltpu.VMEM((4, 32, 128), F32), pltpu.SemaphoreType.DMA((2, 3))]
    return pl.pallas_call(
        grads_kernel,
        out_shape=tuple(jax.ShapeDtypeStruct((32, w), F32) for w in wide),
        in_specs=[VMEM] * 6,
        out_specs=tuple([VMEM] * 6),
        scratch_shapes=scratch,
        compiler_params=params(6),
        name="reduce_grads",
    )(up_res, down_res, *[a.reshape(4, 4, 64, a.shape[1]) for a in (qk, value, out, small)])


def write_kernel(
    up_ref, down_ref, qk_ref, value_ref, out_ref, small_ref,
    o_q, o_k, o_v, o_out, o_up, o_down, o_actor, o_flat,
):
    o_q[...] = qk_ref[:, :256]
    o_k[...] = qk_ref[:, 256:]
    o_v[...] = value_ref[...]
    o_up[...] = up_ref[...]
    o_out[...] = out_ref[...]
    o_down[...] = down_ref[...]
    flat = jnp.transpose(small_ref[...])
    o_actor[...] = flat[:16, :]
    o_flat[...] = flat[16:24, :]


def write_outputs(*parts):
    sd = jax.ShapeDtypeStruct
    return pl.pallas_call(
        write_kernel,
        out_shape=(
            sd((32, 256), F32), sd((32, 256), F32), sd((32, 256), F32), sd((32, 256), F32), sd((32, 1024), F32),
            sd((32, 1024), F32), sd((16, 32), F32), sd((8, 32), F32),
        ),
        in_specs=[VMEM] * 6,
        out_specs=tuple([VMEM] * 8),
        name="write_outputs",
    )(*parts)


def per_device(
    initial_state,
    actions,
    next_state,
    reward_table,
    reward_scale,
    observe_table,
    gain_attn,
    w_query,
    w_key,
    w_value,
    w_out,
    gain_mlp,
    w_up,
    w_down,
    gain_final,
    actor_head,
    critic_head,
):
    token_total = actions.size * lax.axis_size("dp")

    def line(vector):
        return vector.reshape(1, -1)

    qkv, match, mixed, h_table, dx_one_low, grad_heads, final_terms, mlp_terms, up_res, down_res = policy(
        token_total,
        line(initial_state), actions.T, line(reward_scale), next_state.T, reward_table.T, observe_table,
        line(gain_attn), w_query, w_key, w_value, w_out, line(gain_mlp), line(gain_final),
        actor_head.T, line(critic_head), w_up, w_down,
    )
    grad_out = jnp.dot(dx_one_low.T, mixed, preferred_element_type=F32)
    grad_qk, grad_value, small = attend_back(
        dx_one_low, w_out, qkv, match, h_table, observe_table, w_query, w_key, w_value,
        grad_heads, final_terms, mlp_terms,
    )
    parts = reduce_grads(up_res, down_res, grad_qk, grad_value, grad_out, small)
    q, k, v, out, up, down, actor, flat = write_outputs(*parts)
    attn_own = lax.dynamic_slice_in_dim(flat[3], lax.axis_index("mp") * 8, 8, 0)
    return (q, k, v, out.T, up, down.T, attn_own, flat[2], flat[1], actor.T, flat[0])


def solution(mesh):
    return jax.shard_map(
        per_device,
        mesh=mesh,
        in_specs=(
            P("dp"),
            P("dp", None),
            P(),
            P(),
            P("dp"),
            P(),
            P(),
            P(None, "mp"),
            P(None, "mp"),
            P(None, "mp"),
            P("mp", None),
            P(),
            P(None, "mp"),
            P("mp", None),
            P(),
            P(),
            P(),
        ),
        out_specs=(
            P("dp", "mp"),
            P("dp", "mp"),
            P("dp", "mp"),
            P("mp", "dp"),
            P("dp", "mp"),
            P("mp", "dp"),
            P(("dp", "mp")),
            P("dp"),
            P("dp"),
            P("dp", None),
            P("dp"),
        ),
        check_vma=False,
    )
```

time: 279 us -> 226 us (0.81)
  matrix products: 33.9 us -> 2.1 us
  Pallas kernels: 231 us -> 207 us
  local copies, waits for them, and re-layouts: 11.1 us -> 15 us
    dot_general x7 -> x1, matrix products: 33.9 us -> 2.1 us  [per_device(): grad_out = jnp.dot(dx_one_low.T, mixed, preferred_element_type=F32)]
    pallas_call x4 -> x1, Pallas kernels: 159 us -> 141 us  [policy(): pl.pallas_call(functools.partial(policy_kernel, token_total), out_shape=(...]
    pallas_call x1, Pallas kernels: 19.1 us -> 14.5 us  [attend_back(): pl.pallas_call(attend_back_kernel, out_shape=(sd((1024, 512), F32), sd((1...]
    unnamed x25 -> x32, local copies, waits for them, and re-layouts: 9.55 us -> 11.8 us
where the time goes in v1:
time: 226 us; the launch traced here: 224 us
  Pallas kernels  207 us (92%)
  local copies, waits for them, and re-layouts  15 us (7%)
    pallas_call x1, Pallas kernels, policy(): pl.pallas_call(functools.partial(policy_kernel, token_total), out_shape=(...  141 us
    pallas_call x1, Pallas kernels, reduce_grads(): pl.pallas_call(grads_kernel, out_shape=tuple((jax.ShapeDtypeStruct((32, w...  49.5 us
    pallas_call x1, Pallas kernels, attend_back(): pl.pallas_call(attend_back_kernel, out_shape=(sd((1024, 512), F32), sd((1...  14.5 us
    unnamed x32, local copies, waits for them, and re-layouts  11.8 us

profile of v1, /device:TPU:0, one launch (start us, length us, event | category | flops | bytes accessed | tf_op | source)
XLA Modules:
  0.0 224.4 jit_solution(18389097880302392243)
XLA Ops:
  0.6 1.3 reshape.58.critic_ref
  1.9 140.8 %policy.1 = (bf16[1024,768]{1,0:T(8,128)(2,1)}, bf16[1024,256]{1,0:T(8,128)(2,1)}, bf16[1024,256]{1,0:T(8,128)(2,1)}, bf16[256,1024]{1,0:T(8,128)(2,1)}, bf16[10...) custom-call(s32[1,64]{1,0:T(1,128)} %bitcast.37, ...), custom_call_target="tpu_custom_call" | custom-call | tf_op jit(solution)/shard_map/policy/pallas_call | solution.py:663
  142.7 0.0 copy-done.2
  142.7 0.0 copy-start.1
  142.7 1.6 copy-done.1
  144.3 1.0 copy-done.3
  145.4 1.0 copy-done.4
  146.4 1.0 copy-done.5
  147.4 1.0 copy-done.6
  148.5 1.4 copy-done.7
  149.9 1.0 copy-done.10
  150.9 1.0 copy-done.11
  152.0 1.0 copy-done.12
  153.0 0.8 copy-done.13
  153.8 0.8 copy-done.14
  154.5 14.5 %attend_back.1 = (f32[1024,512]{1,0:T(8,128)S(1)}, f32[1024,256]{1,0:T(8,128)S(1)}, f32[1024,128]{1,0:T(8,128)S(1)}) custom-call(bf16[1024,1024]{1,0:T(8,128)(2,1)S(1)} %copy-done.1, bf16[256,1024]{1,0:T(8,128)(2,1)S(1)} %copy-done.6, bf16[1024,768]{1,0:T(8,128)(2,1)S(1)} %copy-done.7, bf16[1024,256]{1,0:T(8,128)(2,1)S(1)} %copy-done.10, ...), custom_call_target="tpu_custom_call" | custom-call | tf_op jit(solution)/shard_map/attend_back/pallas_call | solution.py:752
  169.0 0.0 copy-start
  169.0 0.0 copy-start.8
  169.0 2.1 fusion
  171.1 0.0 copy-done
  171.2 49.5 %reduce_grads.1 = (f32[32,1024]{1,0:T(8,128)}, f32[32,1024]{1,0:T(8,128)}, f32[32,512]{1,0:T(8,128)}, f32[32,256]{1,0:T(8,128)}, f32[32,256]{1,0:T(8,128)}, /*index=5*/f32[32,128]{1,0:T(8,128)}) custom-call(f32[4,64,1024]{2,1,0:T(8,128)} %get-tuple-element.38.refs_0_, f32[4,64,1024]{2,1,0:T(8,128)} %get-tuple-element.39.refs_1_, f32[4,4,64,512]{3,2,1,0:T(8,128)} %bitcast.26, ...), custom_call_target="tpu_custom_call" | custom-call | tf_op jit(solution)/shard_map/reduce_grads/pallas_call | solution.py:852
  220.7 1.7 write_outputs.1
  222.5 1.3 slice_bitcast_fusion
  223.8 0.6 dynamic-slice_bitcast_fusion
  (16 shorter events, 0.0 us)
Async XLA Ops:
  1.9 140.8 %copy-start.2 = (bf16[256,1024]{1,0:T(8,128)(2,1)S(1)}, bf16[256,1024]{1,0:T(8,128)(2,1)}, u32[]{:S(2)}) copy-start(bf16[256,1024]{1,0:T(8,128)(2,1)} %obs_ref.3) | copy-start | bytes 1572868
  142.7 1.6 copy-start.1
  144.3 1.0 copy-start.3
  145.4 1.0 copy-start.4
  146.4 1.0 copy-start.5
  147.4 1.0 copy-start.6
  148.5 1.4 copy-start.7
  149.9 1.0 copy-start.10
  150.9 1.0 copy-start.11
  152.0 1.0 copy-start.12
  153.0 0.8 copy-start.13
  153.8 0.8 copy-start.14
  154.5 14.5 %copy-start.15 = (bf16[1024,256]{1,0:T(8,128)(2,1)S(1)}, bf16[1024,256]{1,0:T(8,128)(2,1)}, u32[]{:S(2)}) copy-start(bf16[1024,256]{1,0:T(8,128)(2,1)} %get-tuple-element.49) | copy-start | bytes 1572868
  169.0 2.1 copy-start
  169.0 2.1 copy-start.8
  169.0 2.1 copy-start.9

commit v2 on v1

--- a/solution.py
+++ b/solution.py
@@ -17,6 +17,7 @@
 SCALE = 1.0 / math.sqrt(HEAD_DIM)
 MESH = pl.DeviceIdType.MESH
 VMEM = pl.BlockSpec(memory_space=pltpu.VMEM)
+WIDE = 1024
 ANY = pl.BlockSpec(memory_space=pl.ANY)
 F32 = jnp.float32
 BF16 = jnp.bfloat16
@@ -342,11 +343,12 @@
     each_block(dst, body)
 
 
-def ring_one(order, src, bufs, sems):
+def ring_one(order, src, bufs, sems, cols=slice(None)):
     x, z, yh = axes_place()
+    every = slice(None)
     if order == "xz":
-        return Ring(lambda j, h: src.at[j, pl.ds(h * 2, 2)], bufs, sems, x, at_x(1), at_x(3))
-    return Ring(lambda j, h: src.at[pl.ds(h * 2, 2), j], bufs, sems, z, at_z(1), at_z(3))
+        return Ring(lambda j, h: src.at[j, pl.ds(h * 2, 2), every, cols], bufs, sems, x, at_x(1), at_x(3))
+    return Ring(lambda j, h: src.at[pl.ds(h * 2, 2), j, every, cols], bufs, sems, z, at_z(1), at_z(3))
 
 
 def ring_two(order, res, bufs, sems):
@@ -391,7 +393,8 @@
     token_total,
     init_ref, act_ref, scale_ref, next_ref, rew_ref, obs_ref, gain_attn, wq_ref, wk_ref, wv_ref, wo_ref,
     gain_mlp, gain_fin, actor_ref, critic_ref, up_hbm, down_hbm,
-    qkv_ref, match_ref, mixed_ref, ht_ref, low_one, gh_ref, g_fin, g_mlp, up_res, down_res,
+    qkv_out, match_out, mixed_out, ht_out, down_out, low_one, gh_ref, g_fin, g_mlp, res_a, res_b,
+    qkv_ref, match_ref, mixed_ref, ht_ref, flush_sem,
     r_init, r_act, r_scale, roll_sem, tables, st_ref, own_ref, head_f, heads,
     w_up, w_down, w_sem,
     p, near_own, near_far, far, whole, h_two, up_rows, hidden, low_two, d_up, x_one, dx_two, buf_a, buf_b,
@@ -400,7 +403,14 @@
     stats, rest = rest[:6], rest[6:]
     sems_a, sems_b, sems_d = rest[0:3], rest[3:6], rest[6:9]
     gs_b, gs_d, gs_e = rest[9:12], rest[12:15], rest[15:18]
-    um, ul, ur, us, dm, dl, dr, ds = rest[18:26]
+    ring_a, ring_b = rest[18:22], rest[22:26]
+    flushed = []
+
+    def flush(src, dst):
+        cp = pltpu.make_async_copy(src, dst, flush_sem.at[len(flushed)])
+        cp.start()
+        flushed.append(cp)
+
     d, m, c, l = place()
     weights = [
         pltpu.make_async_copy(up_hbm, w_up, w_sem.at[0]), pltpu.make_async_copy(down_hbm, w_down, w_sem.at[1]),
@@ -421,6 +431,7 @@
         ht_ref[at, :] = (x * inverse_rms(x) * gain_attn[...]).astype(BF16)
 
     by_blocks(256, 32, table_rows)
+    flush(ht_ref, ht_out)
     for n, w in enumerate((wq_ref, wk_ref, wv_ref)):
         tables[:, n * 256 : (n + 1) * 256] = dot(ht_ref[...], w[...], (1, 0)).astype(BF16)
     head_f[...] = jnp.zeros_like(head_f)
@@ -485,6 +496,9 @@
     attend(1 - c, l)
     sums.give_own()
     attend(c, l)
+    flush(qkv_ref, qkv_out)
+    flush(match_ref, match_out)
+    flush(mixed_ref, mixed_out)
     for h in range(2):
         at = pl.ds(h * 128, 128)
         mine = match_ref[rows(block_at(h, c, l), 128), :]
@@ -516,17 +530,17 @@
 
     def forward(spans):
         def up(j):
-            cols = pl.ds(j, 256)
+            cols = pl.ds(j, WIDE)
             u = dot(spans_of(h_two, spans), w_up[:, cols], (1, 0))
             put_spans(up_rows, spans, cols, u)
             put_spans(hidden, spans, cols, (u / (1.0 + jnp.exp(-u))).astype(BF16))
 
         def down(j):
-            cols = pl.ds(j, 256)
+            cols = pl.ds(j, WIDE)
             put_spans(p, spans, cols, dot(spans_of(hidden, spans), w_down[:, cols], (1, 0)))
 
-        by_blocks(1024, 256, up)
-        by_blocks(1024, 256, down)
+        by_blocks(1024, WIDE, up)
+        by_blocks(1024, WIDE, down)
 
     sums = Sums(p, near_own, near_far, far, sems_b)
     gather_work_sum(gather, sums, forward)
@@ -595,18 +609,18 @@
 
     def backward(spans):
         def up(j):
-            cols = pl.ds(j, 256)
+            cols = pl.ds(j, WIDE)
             d_hidden = dot(spans_of(low_two, spans), w_down[cols, :], (1, 1)).astype(BF16).astype(F32)
             u = spans_of(up_rows, spans, cols)
             sig = 1.0 / (1.0 + jnp.exp(-u))
             put_spans(d_up, spans, cols, (d_hidden * sig * (1.0 + u * (1.0 - sig))).astype(BF16))
 
         def down(j):
-            cols = pl.ds(j, 256)
+            cols = pl.ds(j, WIDE)
             put_spans(p, spans, cols, dot(spans_of(d_up, spans), w_up[cols, :], (1, 1)))
 
-        by_blocks(1024, 256, up)
-        by_blocks(1024, 256, down)
+        by_blocks(1024, WIDE, up)
+        by_blocks(1024, WIDE, down)
 
     sums = Sums(p, near_own, near_far, far, sems_d)
     gather_work_sum(gather, sums, backward)
@@ -619,12 +633,15 @@
 
         lax.fori_loop(0, 4, tile, 0)
 
-    up_ring = ring_one("xz", grad_up, (um, ul, ur), us)
-    down_ring = ring_one("zx", grad_down, (dm, dl, dr), ds)
+    rings = [
+        ring_one("xz", grad_up, ring_a[:3], ring_a[3], pl.ds(0, 512)),
+        ring_one("zx", grad_up, ring_b[:3], ring_b[3], pl.ds(512, 512)),
+    ]
     weight_grad(grad_up, h_two, d_up)
-    up_ring.start()
+    for ring in rings:
+        ring.start()
     weight_grad(grad_down, low_two, hidden)
-    down_ring.start()
+    flush(grad_down, down_out)
     gather.drain()
 
     gather = Gather(buf_b, whole, low_one, gs_e)
@@ -645,17 +662,19 @@
         gather.take_core(h, k)
     for h in range(2):
         gather.take_far(h, 0)
-    up_ring.middle()
-    down_ring.middle()
+    for ring in rings:
+        ring.middle()
     for h in range(2):
         gather.take_far(h, 1)
     for h, k in CHUNKS:
         gather.take_fwd(h, k)
     gather.drain()
-    up_ring.finish(lambda h: up_res.at[pl.ds(h * 2, 2)])
-    down_ring.finish(lambda h: down_res.at[pl.ds(h * 2, 2)])
-    up_ring.drain()
-    down_ring.drain()
+    for ring, res in zip(rings, (res_a, res_b)):
+        ring.finish(lambda h, res=res: res.at[pl.ds(h * 2, 2)])
+    for ring in rings:
+        ring.drain()
+    for cp in flushed:
+        cp.wait()
 
 
 def policy(token_total, *args):
@@ -664,12 +683,14 @@
         functools.partial(policy_kernel, token_total),
         out_shape=(
             sd((1024, 768), BF16), sd((1024, 256), BF16), sd((1024, 256), BF16), sd((256, 1024), BF16),
-            sd((1024, 1024), BF16), sd((1024, 128), F32), sd((8, 1024), F32), sd((8, 1024), F32),
-            sd((4, 64, 1024), F32), sd((4, 64, 1024), F32),
+            sd((4, 4, 64, 1024), F32), sd((1024, 1024), BF16), sd((1024, 128), F32), sd((8, 1024), F32),
+            sd((8, 1024), F32), sd((4, 64, 512), F32), sd((4, 64, 512), F32),
         ),
         in_specs=[VMEM] * 15 + [ANY] * 2,
-        out_specs=tuple([VMEM] * 10),
+        out_specs=tuple([ANY] * 5 + [VMEM] * 6),
         scratch_shapes=[
+            vm((1024, 768), BF16), vm((1024, 256), BF16), vm((1024, 256), BF16), vm((256, 1024), BF16),
+            pltpu.SemaphoreType.DMA((5,)),
             vm((1, 64), jnp.int32), vm((16, 64), jnp.int32), vm((1, 64), F32), pltpu.SemaphoreType.DMA((2, 3)),
             vm((256, 768), BF16), vm((16, 64), F32), vm((256, 128), F32), vm((32, 1024), F32), vm((128, 1024), BF16),
             vm((1024, 1024), BF16), vm((1024, 1024), BF16), pltpu.SemaphoreType.DMA((2,)),
@@ -679,7 +700,7 @@
             vm((256, 1024), F32), vm((256, 1024), F32), vm((256, 1024), F32), vm((256, 1024), F32),
             vm((256, 1024), BF16), vm((4, 4, 64, 1024), F32), vm((4, 4, 64, 1024), F32),
             *STATS_SCRATCH, *SUM_SEMS, *SUM_SEMS, *SUM_SEMS, *GATHER_SEMS, *GATHER_SEMS, *GATHER_SEMS,
-            *one_scratch(1024), *one_scratch(1024),
+            *one_scratch(512), *one_scratch(512),
         ],
         compiler_params=params(1),
         name="policy",
@@ -691,10 +712,79 @@
     return high, (value - high.astype(F32)).astype(BF16)
 
 
-def attend_back_kernel(
-    dx_ref, wo_ref, qkv_ref, match_ref, ht_ref, obs_ref, wq_ref, wk_ref, wv_ref, gh_ref, gf_ref, gm_ref,
-    qk_ref, v_ref, small_ref, sums, dt_ref, vec_ref,
-):
+UP_A, UP_B, DOWN_A, DOWN_B, OUT, QK, VALUE, SMALL = range(8)
+ORDER = ("xz", "zx", "xz", "zx", "zx", "xz", "zx", "xz")
+WIDTH = (512, 512, 512, 512, 256, 512, 256, 128)
+LOADS = ((4, 4, 64, 1024), F32), ((1024, 1024), BF16), ((1024, 256), BF16), ((256, 1024), BF16), \
+    ((1024, 768), BF16), ((1024, 256), BF16), ((256, 1024), BF16), ((256, 1024), BF16), \
+    ((1024, 256), BF16), ((1024, 256), BF16), ((1024, 256), BF16), ((1024, 128), F32), \
+    ((8, 1024), F32), ((8, 1024), F32), ((4, 64, 512), F32), ((4, 64, 512), F32)
+
+
+def tail_kernel(*refs):
+    n = len(LOADS)
+    hbm, outs, held, rest = refs[:n], refs[n : n + 8], refs[n + 8 : 2 * n + 8], refs[2 * n + 8 :]
+    load_sem, qk_ref, v_ref, out_ref, sums, dt_ref, vec_ref, mp_buf, mp_sem = rest[:9]
+    rest = rest[9:]
+    down_ref, dx_ref, mixed_ref, wo_ref, qkv_ref, match_ref, ht_ref, obs_ref = held[:8]
+    wq_ref, wk_ref, wv_ref, small_ref, gf_ref, gm_ref, res_a, res_b = held[8:]
+    loads = [pltpu.make_async_copy(a, b, load_sem.at[k]) for k, (a, b) in enumerate(zip(hbm, held))]
+    for k in (14, 15, 0, *range(1, 14)):
+        loads[k].start()
+    d, m, c, l = place()
+    x, z, yh = axes_place()
+    yother = (d + 1 - 2 * yh, m)
+    peers = [(d, lax.rem(m + j, 4)) for j in (1, 2, 3)]
+    greet([at_x(1), at_x(3), at_z(1), at_z(3), yother] + peers)
+
+    first, second, results, ends = {}, [], [res_a, res_b], []
+    sources = {
+        DOWN_A: (down_ref, pl.ds(0, 512)), DOWN_B: (down_ref, pl.ds(512, 512)), OUT: (out_ref, slice(None)),
+        QK: (qk_ref, slice(None)), VALUE: (v_ref, slice(None)), SMALL: (small_ref, slice(None)),
+    }
+    for i in range(2, 8):
+        mid, fl, fr, sems, res = rest[:5]
+        rest = rest[5:]
+        src, cols = sources[i]
+        if i == SMALL:
+            src = rest[0]
+            small4 = src
+            rest = rest[1:]
+        first[i] = ring_one(ORDER[i], src, (mid, fl, fr), sems, cols)
+        results.append(res)
+    for i in range(8):
+        mid, fl, fr, res, ybuf, sems, ysem = rest[:7]
+        rest = rest[7:]
+        second.append(ring_two(ORDER[i], results[i], (mid, fl, fr), sems))
+        ends.append((res, ybuf, ysem))
+    tails = {}
+
+    def turn(i):
+        first[i].finish(lambda h: results[i].at[pl.ds(h * 2, 2)])
+        second[i].start()
+
+    def send_tail(i):
+        res, ybuf, ysem = ends[i]
+        second[i].finish(lambda h: res.at[pl.ds(h * 32, 32)])
+        tails[i] = remote(res.at[rows((1 - yh) * 32, 32)], ybuf, ysem, (), yother)
+
+    loads[14].wait()
+    loads[15].wait()
+    second[UP_A].start()
+    second[UP_B].start()
+    loads[0].wait()
+    first[DOWN_A].start()
+    first[DOWN_B].start()
+    for k in range(1, 14):
+        loads[k].wait()
+
+    def out_tile(j, carry):
+        cols = rows(j * 256, 256)
+        out_ref[j] = dot(dx_ref[:, cols], mixed_ref[...], (0, 0)).reshape(4, 64, 256)
+        return carry
+
+    lax.fori_loop(0, 4, out_tile, 0)
+    first[OUT].start()
     sums[...] = jnp.zeros_like(sums)
 
     def block(b, carry):
@@ -717,14 +807,25 @@
         sums[...] += dot(match_ref[at, :], d_qkv, (0, 0))
         return carry
 
-    lax.fori_loop(0, 8, block, 0)
+    lax.fori_loop(0, 4, block, 0)
+    for i in (UP_A, UP_B):
+        second[i].middle()
+    for i in (DOWN_A, DOWN_B):
+        first[i].middle()
+    lax.fori_loop(4, 8, block, 0)
     high, low = halves(sums[...])
-    for i in range(4):
-        cols = pl.ds(i * 256, 256)
+
+    def grad_tile(j, carry):
+        cols = rows(j * 256, 256)
         table = ht_ref[:, cols]
         total = dot(table, high, (0, 0)) + dot(table, low, (0, 0))
-        qk_ref[cols, :] = total[:, :512]
-        v_ref[cols, :] = total[:, 512:]
+        qk_ref[j] = total[:, :512].reshape(4, 64, 512)
+        v_ref[j] = total[:, 512:].reshape(4, 64, 256)
+        return carry
+
+    lax.fori_loop(0, 4, grad_tile, 0)
+    first[QK].start()
+    first[VALUE].start()
     dt_ref[...] = jnp.zeros_like(dt_ref)
     for n, w in enumerate((wq_ref, wk_ref, wv_ref)):
         cols = slice(n * 256, (n + 1) * 256)
@@ -736,78 +837,35 @@
     def gain_rows(i):
         at = pl.ds(i, 32)
         x = obs_ref[at, :].astype(F32)
-        inv = lax.rsqrt(jnp.mean(x * x, axis=-1, keepdims=True) + EPS)
-        vec_ref[16:24] += fold8(dt_ref[at, :] * x * inv)
+        vec_ref[16:24] += fold8(dt_ref[at, :] * x * inverse_rms(x))
 
     by_blocks(256, 32, gain_rows)
     place_at = (iota((32, 128), 1) == 17 + iota((32, 128), 0) // 8).astype(BF16)
     vec = vec_ref[...]
     high, low = halves(vec)
     lowest = (vec - high.astype(F32) - low.astype(F32)).astype(BF16)
-    small_ref[...] = gh_ref[...] + sum(dot(part, place_at, (0, 0)) for part in (high, low, lowest))
-
-
-def attend_back(*args):
-    sd = jax.ShapeDtypeStruct
-    return pl.pallas_call(
-        attend_back_kernel,
-        out_shape=(sd((1024, 512), F32), sd((1024, 256), F32), sd((1024, 128), F32)),
-        in_specs=[VMEM] * 12,
-        out_specs=tuple([VMEM] * 3),
-        scratch_shapes=[pltpu.VMEM((256, 768), F32), pltpu.VMEM((256, 1024), F32), pltpu.VMEM((32, 1024), F32)],
-        compiler_params=pltpu.CompilerParams(vmem_limit_bytes=40 * 1024 * 1024),
-        name="attend_back",
-    )(*args)
-
-
-FIRST = ("xz", "zx", "zx", "xz")
-SECOND = ("xz", "zx") + FIRST
-
-
-def grads_kernel(*refs):
-    ins, outs, scratch = refs[:6], refs[6:12], refs[12:]
-    mp_buf, mp_sem = scratch[-2:]
-    d, m, c, l = place()
-    x, z, yh = axes_place()
-    yother = (d + 1 - 2 * yh, m)
-    peers = [(d, lax.rem(m + j, 4)) for j in (1, 2, 3)]
-    greet([at_x(1), at_x(3), at_z(1), at_z(3), yother] + peers)
-
-    first, second, results = [], [], [ins[0], ins[1]]
-    for i, order in enumerate(FIRST):
-        mid, fl, fr, sems, res = scratch[5 * i : 5 * i + 5]
-        first.append(ring_one(order, ins[2 + i], (mid, fl, fr), sems))
-        results.append(res)
-    at = 20
-    ends = []
-    for i, order in enumerate(SECOND):
-        mid, fl, fr, res, ybuf, sems, ysem = scratch[at + 7 * i : at + 7 * i + 7]
-        second.append(ring_two(order, results[i], (mid, fl, fr), sems))
-        ends.append((res, ybuf, ysem))
-    tails = []
-
-    def send_tail(i):
-        res, ybuf, ysem = ends[i]
-        second[i].finish(lambda h: res.at[pl.ds(h * 32, 32)])
-        tails.append(remote(res.at[rows((1 - yh) * 32, 32)], ybuf, ysem, (), yother))
-
-    for ring in first:
-        ring.start()
-    for ring in second[:2]:
-        ring.start()
-    for ring in first:
-        ring.middle()
-    for ring in second[:2]:
-        ring.middle()
-    for i, ring in enumerate(first):
-        res = results[2 + i]
-        ring.finish(lambda h, res=res: res.at[pl.ds(h * 2, 2)])
-        second[2 + i].start()
-    for i in range(2):
-        send_tail(i)
-    for ring in second[2:]:
-        ring.middle()
-    for i in (5, 2, 3, 4):
+    small = small_ref[...] + sum(dot(part, place_at, (0, 0)) for part in (high, low, lowest))
+    small4[...] = small.reshape(4, 4, 64, 128)
+    first[SMALL].start()
+
+    first[OUT].middle()
+    send_tail(UP_A)
+    send_tail(UP_B)
+    turn(DOWN_A)
+    turn(DOWN_B)
+    for i in (QK, VALUE, SMALL):
+        first[i].middle()
+    turn(OUT)
+    second[DOWN_A].middle()
+    second[DOWN_B].middle()
+    for i in (QK, VALUE, SMALL):
+        turn(i)
+    send_tail(DOWN_A)
+    send_tail(DOWN_B)
+    second[OUT].middle()
+    for i in (QK, VALUE, SMALL):
+        second[i].middle()
+    for i in (OUT, SMALL, QK, VALUE):
         send_tail(i)
 
     def total(i, put):
@@ -824,67 +882,75 @@
         mp_buf[m, pl.ds(k, 8), :] = value
 
     shares = []
-    for n, i in enumerate((0, 1, 5, 2, 3, 4)):
-        tails[n].wait_recv()
-        if i == 5:
+    for i in (UP_A, UP_B, DOWN_A, DOWN_B, OUT, SMALL, QK, VALUE):
+        tails[i].wait_recv()
+        if i == SMALL:
             total(i, to_mp)
-            for j, dev in enumerate(peers):
-                shares.append(remote(mp_buf.at[m], mp_buf.at[m], mp_sem, (j,), dev))
+            shares = [remote(mp_buf.at[m], mp_buf.at[m], mp_sem, (j,), dev) for j, dev in enumerate(peers)]
         else:
             total(i, to_out(outs[i]))
     for cp in shares:
         cp.wait_recv()
-    outs[5][...] = mp_buf[0] + mp_buf[1] + mp_buf[2] + mp_buf[3]
-    for cp in shares + tails:
+    outs[SMALL][...] = mp_buf[0] + mp_buf[1] + mp_buf[2] + mp_buf[3]
+    for cp in [*shares, *tails.values()]:
         cp.wait_send()
-    for ring in first + second:
+    for ring in [*first.values(), *second]:
         ring.drain()
 
 
-def reduce_grads(up_res, down_res, qk, value, out, small):
-    wide = [1024, 1024, 512, 256, 256, 128]
-    scratch = []
-    for w in wide[2:]:
-        scratch += one_scratch(w) + [pltpu.VMEM((4, 64, w), F32)]
-    for w in wide:
-        scratch += two_scratch(w)
-    scratch += [pltpu.VMEM((4, 32, 128), F32), pltpu.SemaphoreType.DMA((2, 3))]
+def tail(*args):
+    vm, dma = pltpu.VMEM, pltpu.SemaphoreType.DMA
+    scratch = [vm(shape, kind) for shape, kind in LOADS]
+    scratch += [
+        dma((len(LOADS),)), vm((4, 4, 64, 512), F32), vm((4, 4, 64, 256), F32), vm((4, 4, 64, 256), F32),
+        vm((256, 768), F32), vm((256, 1024), F32), vm((32, 1024), F32), vm((4, 32, 128), F32), dma((2, 3)),
+    ]
+    for i in range(2, 8):
+        scratch += one_scratch(WIDTH[i]) + [vm((4, 64, WIDTH[i]), F32)]
+        if i == SMALL:
+            scratch += [vm((4, 4, 64, 128), F32)]
+    for i in range(8):
+        scratch += two_scratch(WIDTH[i])
     return pl.pallas_call(
-        grads_kernel,
-        out_shape=tuple(jax.ShapeDtypeStruct((32, w), F32) for w in wide),
-        in_specs=[VMEM] * 6,
-        out_specs=tuple([VMEM] * 6),
+        tail_kernel,
+        out_shape=tuple(jax.ShapeDtypeStruct((32, w), F32) for w in WIDTH),
+        in_specs=[ANY] * len(LOADS),
+        out_specs=tuple([VMEM] * 8),
         scratch_shapes=scratch,
-        compiler_params=params(6),
-        name="reduce_grads",
-    )(up_res, down_res, *[a.reshape(4, 4, 64, a.shape[1]) for a in (qk, value, out, small)])
+        compiler_params=params(2),
+        name="tail",
+    )(*args)
 
 
 def write_kernel(
-    up_ref, down_ref, qk_ref, value_ref, out_ref, small_ref,
-    o_q, o_k, o_v, o_out, o_up, o_down, o_actor, o_flat,
+    up_a, up_b, down_a, down_b, out_ref, qk_ref, value_ref, small_ref,
+    o_q, o_k, o_v, o_out, o_up, o_down, o_actor, o_critic, o_final, o_mlp, o_attn,
 ):
     o_q[...] = qk_ref[:, :256]
     o_k[...] = qk_ref[:, 256:]
     o_v[...] = value_ref[...]
-    o_up[...] = up_ref[...]
+    o_up[:, :512] = up_a[...]
+    o_up[:, 512:] = up_b[...]
     o_out[...] = out_ref[...]
-    o_down[...] = down_ref[...]
+    o_down[:, :512] = down_a[...]
+    o_down[:, 512:] = down_b[...]
     flat = jnp.transpose(small_ref[...])
     o_actor[...] = flat[:16, :]
-    o_flat[...] = flat[16:24, :]
+    o_critic[...] = flat[16:17, :]
+    o_final[...] = flat[17:18, :]
+    o_mlp[...] = flat[18:19, :]
+    own = jnp.transpose(small_ref[rows(lax.axis_index("mp") * 8, 8), :])
+    o_attn[...] = own[19:20, :]
 
 
 def write_outputs(*parts):
     sd = jax.ShapeDtypeStruct
+    shapes = [(32, 256)] * 4 + [(32, 1024)] * 2 + [(16, 32)] + [(1, 32)] * 3 + [(1, 8)]
     return pl.pallas_call(
         write_kernel,
-        out_shape=(
-            sd((32, 256), F32), sd((32, 256), F32), sd((32, 256), F32), sd((32, 256), F32), sd((32, 1024), F32),
-            sd((32, 1024), F32), sd((16, 32), F32), sd((8, 32), F32),
-        ),
-        in_specs=[VMEM] * 6,
-        out_specs=tuple([VMEM] * 8),
+        out_shape=tuple(sd(shape, F32) for shape in shapes),
+        in_specs=[VMEM] * 8,
+        out_specs=tuple([VMEM] * 11),
         name="write_outputs",
     )(*parts)
 
@@ -913,21 +979,21 @@
     def line(vector):
         return vector.reshape(1, -1)
 
-    qkv, match, mixed, h_table, dx_one_low, grad_heads, final_terms, mlp_terms, up_res, down_res = policy(
+    qkv, match, mixed, h_table, grad_down, dx_one_low, grad_heads, final_terms, mlp_terms, res_a, res_b = policy(
         token_total,
         line(initial_state), actions.T, line(reward_scale), next_state.T, reward_table.T, observe_table,
         line(gain_attn), w_query, w_key, w_value, w_out, line(gain_mlp), line(gain_final),
         actor_head.T, line(critic_head), w_up, w_down,
     )
-    grad_out = jnp.dot(dx_one_low.T, mixed, preferred_element_type=F32)
-    grad_qk, grad_value, small = attend_back(
-        dx_one_low, w_out, qkv, match, h_table, observe_table, w_query, w_key, w_value,
-        grad_heads, final_terms, mlp_terms,
+    parts = tail(
+        grad_down, dx_one_low, mixed, w_out, qkv, match, h_table, observe_table, w_query, w_key, w_value,
+        grad_heads, final_terms, mlp_terms, res_a, res_b,
     )
-    parts = reduce_grads(up_res, down_res, grad_qk, grad_value, grad_out, small)
-    q, k, v, out, up, down, actor, flat = write_outputs(*parts)
-    attn_own = lax.dynamic_slice_in_dim(flat[3], lax.axis_index("mp") * 8, 8, 0)
-    return (q, k, v, out.T, up, down.T, attn_own, flat[2], flat[1], actor.T, flat[0])
+    q, k, v, out, up, down, actor, critic, final, mlp, attn = write_outputs(*parts)
+    return (
+        q, k, v, out.T, up, down.T, attn.reshape(-1), mlp.reshape(-1), final.reshape(-1), actor.T,
+        critic.reshape(-1),
+    )
 
 
 def solution(mesh):

time: 226 us -> 184 us (0.81)
  Pallas kernels: 207 us -> 181 us
  local copies, waits for them, and re-layouts: 15 us -> 1.28 us
    pallas_call x1, Pallas kernels: 141 us -> 114 us  [policy(): pl.pallas_call(functools.partial(policy_kernel, token_total), out_shape=(...]
    unnamed x32 -> x0, local copies, waits for them, and re-layouts: 11.8 us -> none
    pallas_call x3 -> x2, Pallas kernels: 65.8 us -> 67.3 us  [the longest x1 65.5 us: tail(): pl.pallas_call(tail_kernel, out_shape=tuple((jax.ShapeDtypeStruct((32, w)...]
where the time goes in v2:
time: 184 us; the launch traced here: 183 us
  Pallas kernels  181 us (98%)
    pallas_call x1, Pallas kernels, policy(): pl.pallas_call(functools.partial(policy_kernel, token_total), out_shape=(...  114 us
    pallas_call x1, Pallas kernels, tail(): pl.pallas_call(tail_kernel, out_shape=tuple((jax.ShapeDtypeStruct((32, w)...  65.5 us

profile of v2, /device:TPU:0, one launch (start us, length us, event | category | flops | bytes accessed | tf_op | source)
XLA Modules:
  0.0 183.0 jit_solution(18401859549421464800)
XLA Ops:
  0.6 1.3 reshape.57.critic_ref
  1.9 113.6 %policy.1 = (bf16[1024,768]{1,0:T(8,128)(2,1)}, bf16[1024,256]{1,0:T(8,128)(2,1)}, bf16[1024,256]{1,0:T(8,128)(2,1)}, bf16[256,1024]{1,0:T(8,128)(2,1)}, f32[4,4...) custom-call(s32[1,64]{1,0:T(1,128)} %bitcast.23, ...), custom_call_target="tpu_custom_call" | custom-call | tf_op jit(solution)/shard_map/policy/pallas_call | solution.py:682
  115.6 65.5 %tail.1 = (f32[32,512]{1,0:T(8,128)}, f32[32,512]{1,0:T(8,128)}, f32[32,512]{1,0:T(8,128)}, f32[32,512]{1,0:T(8,128)}, f32[32,256]{1,0:T(8,128)}, /*index=5*/f32...) custom-call(f32[4,4,64,1024]{3,2,1,0:T(8,128)} %get-tuple-element.41.refs_0_, ...), custom_call_target="tpu_custom_call" | custom-call | tf_op jit(solution)/shard_map/tail/pallas_call | solution.py:914
  181.1 1.8 write_outputs.1

commit v3 on v2

--- a/solution.py
+++ b/solution.py
@@ -54,12 +54,14 @@
 def stats_devices():
     d, m, c, l = place()
     x, z, yh = axes_place()
-    mine = yh * 4 + m
-    ydev = []
+    plane, column = [], []
+    for j in range(1, 16):
+        other = lax.rem(x * 4 + z + j, 16)
+        plane.append(((other // 4) * 8 + (other % 4) * 2 + yh, m))
     for j in range(1, 8):
-        other = lax.rem(mine + j, 8)
-        ydev.append((x * 8 + z * 2 + other // 4, other % 4))
-    return [at_x(j) for j in (1, 2, 3)], [at_z(j) for j in (1, 2, 3)], ydev
+        other = lax.rem(yh * 4 + m + j, 8)
+        column.append((x * 8 + z * 2 + other // 4, other % 4))
+    return plane, column
 
 
 def greet(devices):
@@ -252,14 +254,15 @@
         done += n
 
 
-def sum_everywhere(value, xs, zs, ys, xsem, zsem, ysem):
+def sum_everywhere(value, between, ps, cs, psem, csem):
     d, m, c, l = place()
     x, z, yh = axes_place()
-    xdev, zdev, ydev = stats_devices()
-
-    def stage(slots, sems, devs, me, value):
+    plane, column = stats_devices()
+
+    def stage(slots, sems, devs, me, value, between=None):
         slots[me] = value
         copies = [remote(slots.at[me], slots.at[me], sems, (j,), dev) for j, dev in enumerate(devs)]
+        done = between() if between is not None else None
         for cp in copies:
             cp.wait_recv()
         total = slots[0]
@@ -267,19 +270,16 @@
             total = total + slots[k]
         for cp in copies:
             cp.wait_send()
-        return total
-
-    value = stage(xs, xsem, xdev, x, value)
-    value = stage(zs, zsem, zdev, z, value)
-    return stage(ys, ysem, ydev, yh * 4 + m, value)
+        return total, done
+
+    value, done = stage(ps, psem, plane, x * 4 + z, value, between)
+    return stage(cs, csem, column, yh * 4 + m, value)[0], done
 
 
 STATS_SCRATCH = [
-    pltpu.VMEM((4, 8, 128), F32),
-    pltpu.VMEM((4, 8, 128), F32),
+    pltpu.VMEM((16, 8, 128), F32),
     pltpu.VMEM((8, 8, 128), F32),
-    pltpu.SemaphoreType.DMA((2, 3)),
-    pltpu.SemaphoreType.DMA((2, 3)),
+    pltpu.SemaphoreType.DMA((2, 15)),
     pltpu.SemaphoreType.DMA((2, 7)),
 ]
 
@@ -322,11 +322,12 @@
 
 
 def each_block(ref, body):
+    n = min(16, ref.shape[-2])
     if len(ref.shape) == 3:
         for k in range(ref.shape[0]):
-            by_blocks(ref.shape[1], 16, lambda i, k=k: body((k, pl.ds(i, 16), slice(None))))
+            by_blocks(ref.shape[1], n, lambda i, k=k: body((k, pl.ds(i, n), slice(None))))
     else:
-        by_blocks(ref.shape[0], 16, lambda i: body((pl.ds(i, 16), slice(None))))
+        by_blocks(ref.shape[0], n, lambda i: body((pl.ds(i, n), slice(None))))
 
 
 def add_into(dst, src):
@@ -354,23 +355,25 @@
 def ring_two(order, res, bufs, sems):
     x, z, yh = axes_place()
 
+    half = res.shape[1] // 2
+
     def src(j, h):
-        return res.at[j, pl.ds(h * 32, 32)]
+        return res.at[j, pl.ds(h * half, half)]
 
     if order == "xz":
         return Ring(src, bufs, sems, z, at_z(1), at_z(3))
     return Ring(src, bufs, sems, x, at_x(1), at_x(3))
 
 
-def one_scratch(w):
-    return [pltpu.VMEM((2, 2, 64, w), F32)] * 3 + [pltpu.SemaphoreType.DMA((2, 6))]
-
-
-def two_scratch(w):
+def one_scratch(w, part=64):
+    return [pltpu.VMEM((2, 2, part, w), F32)] * 3 + [pltpu.SemaphoreType.DMA((2, 6))]
+
+
+def two_scratch(w, part=64, kept=32):
     return [
-        *[pltpu.VMEM((2, 32, w), F32)] * 3,
-        pltpu.VMEM((64, w), F32),
-        pltpu.VMEM((32, w), F32),
+        *[pltpu.VMEM((2, part // 2, w), F32)] * 3,
+        pltpu.VMEM((part, w), F32),
+        pltpu.VMEM((kept, w), F32),
         pltpu.SemaphoreType.DMA((2, 6)),
         pltpu.SemaphoreType.DMA((2,)),
     ]
@@ -400,7 +403,7 @@
     p, near_own, near_far, far, whole, h_two, up_rows, hidden, low_two, d_up, x_one, dx_two, buf_a, buf_b,
     fin_ref, grad_up, grad_down, *rest,
 ):
-    stats, rest = rest[:6], rest[6:]
+    stats, rest = rest[:4], rest[4:]
     sems_a, sems_b, sems_d = rest[0:3], rest[3:6], rest[6:9]
     gs_b, gs_d, gs_e = rest[9:12], rest[12:15], rest[15:18]
     ring_a, ring_b = rest[18:22], rest[22:26]
@@ -417,8 +420,8 @@
     ]
     for cp in weights:
         cp.start()
-    xdev, zdev, ydev = stats_devices()
-    greet(xdev + zdev + ydev)
+    plane, column = stats_devices()
+    greet(plane + column)
     far_dev = partners()[2]
     copies = [
         remote(src, dst, roll_sem, (n,), far_dev)
@@ -484,7 +487,7 @@
             p[at, :] = dot(mixed, wo_ref[...], (1, 0))
             return carry
 
-        lax.fori_loop(0, 2, block, 0)
+        lax.fori_loop(0, 2, block, 0, unroll=True)
 
     sums = Sums(p, near_own, near_far, far, sems_a)
     attend(1 - c, 1 - l)
@@ -574,20 +577,24 @@
         jnp.sum(advantage, axis=0, keepdims=True),
         jnp.sum(advantage * advantage, axis=0, keepdims=True),
     )
-    totals = sum_everywhere(tile, *stats)
+    real = lane < 16
+    factor = 1.0 / math.sqrt(token_total)
+
+    def policy_terms():
+        logits = jnp.where(real, both, 0.0)
+        mass = jnp.sum(jnp.where(real, jnp.exp(logits), 0.0), axis=1, keepdims=True)
+        logp = jnp.where(real, logits - jnp.log(mass), 0.0)
+        chance = jnp.where(real, jnp.exp(logp), 0.0)
+        entropy = -jnp.sum(chance * logp, axis=1, keepdims=True)
+        picked = jnp.where(real, own, 0.0)
+        d_value = (factor * VALUE_COEF) * (critic - returns)
+        return picked - chance, ENTROPY_COEF * chance * (logp + entropy), d_value
+
+    totals, (push, calm, d_value) = sum_everywhere(tile, policy_terms, *stats)
     mean = totals[0:1, :] * (1.0 / token_total)
     variance = totals[1:2, :] * (1.0 / token_total) - mean * mean
     normed = (advantage - mean) * lax.rsqrt(variance + EPS)
-    real = lane < 16
-    logits = jnp.where(real, both, 0.0)
-    mass = jnp.sum(jnp.where(real, jnp.exp(logits), 0.0), axis=1, keepdims=True)
-    logp = jnp.where(real, logits - jnp.log(mass), 0.0)
-    chance = jnp.where(real, jnp.exp(logp), 0.0)
-    entropy = -jnp.sum(chance * logp, axis=1, keepdims=True)
-    factor = 1.0 / math.sqrt(token_total)
-    picked = jnp.where(real, own, 0.0)
-    d_logits = factor * (-normed * (picked - chance) + ENTROPY_COEF * chance * (logp + entropy))
-    d_value = (factor * VALUE_COEF) * (critic - returns)
+    d_logits = factor * (-normed * push + calm)
     d_both = jnp.where(real, d_logits, jnp.where(lane == 16, d_value, 0.0)).astype(BF16)
     buf_a[...] = dot(d_both, heads[...], (1, 0))
     g_fin[...] = jnp.zeros_like(g_fin)
@@ -712,9 +719,10 @@
     return high, (value - high.astype(F32)).astype(BF16)
 
 
-UP_A, UP_B, DOWN_A, DOWN_B, OUT, QK, VALUE, SMALL = range(8)
-ORDER = ("xz", "zx", "xz", "zx", "zx", "xz", "zx", "xz")
-WIDTH = (512, 512, 512, 512, 256, 512, 256, 128)
+UP_A, UP_B, DOWN_A, DOWN_B, OUT, SMALL, SUM_A, SUM_B = range(8)
+ORDER = ("xz", "zx", "xz", "zx", "zx", "xz", "xz", "zx")
+WIDTH = (512, 512, 512, 512, 256, 128, 384, 384)
+PART = (64, 64, 64, 64, 64, 64, 16, 16)
 LOADS = ((4, 4, 64, 1024), F32), ((1024, 1024), BF16), ((1024, 256), BF16), ((256, 1024), BF16), \
     ((1024, 768), BF16), ((1024, 256), BF16), ((256, 1024), BF16), ((256, 1024), BF16), \
     ((1024, 256), BF16), ((1024, 256), BF16), ((1024, 256), BF16), ((1024, 128), F32), \
@@ -723,9 +731,9 @@
 
 def tail_kernel(*refs):
     n = len(LOADS)
-    hbm, outs, held, rest = refs[:n], refs[n : n + 8], refs[n + 8 : 2 * n + 8], refs[2 * n + 8 :]
-    load_sem, qk_ref, v_ref, out_ref, sums, dt_ref, vec_ref, mp_buf, mp_sem = rest[:9]
-    rest = rest[9:]
+    hbm, outs, held, rest = refs[:n], refs[n : n + 7], refs[n + 7 : 2 * n + 7], refs[2 * n + 7 :]
+    load_sem, out_ref, sums, sums4, full_a, full_b, near_sem, far_sem, mine_ref, dt_ref, vec_ref, small4, mp_buf, mp_sem = rest[:14]
+    rest = rest[14:]
     down_ref, dx_ref, mixed_ref, wo_ref, qkv_ref, match_ref, ht_ref, obs_ref = held[:8]
     wq_ref, wk_ref, wv_ref, small_ref, gf_ref, gm_ref, res_a, res_b = held[8:]
     loads = [pltpu.make_async_copy(a, b, load_sem.at[k]) for k, (a, b) in enumerate(zip(hbm, held))]
@@ -740,16 +748,12 @@
     first, second, results, ends = {}, [], [res_a, res_b], []
     sources = {
         DOWN_A: (down_ref, pl.ds(0, 512)), DOWN_B: (down_ref, pl.ds(512, 512)), OUT: (out_ref, slice(None)),
-        QK: (qk_ref, slice(None)), VALUE: (v_ref, slice(None)), SMALL: (small_ref, slice(None)),
+        SMALL: (small4, slice(None)), SUM_A: (sums4, pl.ds(0, 384)), SUM_B: (sums4, pl.ds(384, 384)),
     }
     for i in range(2, 8):
         mid, fl, fr, sems, res = rest[:5]
         rest = rest[5:]
         src, cols = sources[i]
-        if i == SMALL:
-            src = rest[0]
-            small4 = src
-            rest = rest[1:]
         first[i] = ring_one(ORDER[i], src, (mid, fl, fr), sems, cols)
         results.append(res)
     for i in range(8):
@@ -765,8 +769,10 @@
 
     def send_tail(i):
         res, ybuf, ysem = ends[i]
-        second[i].finish(lambda h: res.at[pl.ds(h * 32, 32)])
-        tails[i] = remote(res.at[rows((1 - yh) * 32, 32)], ybuf, ysem, (), yother)
+        half = res.shape[0] // 2
+        second[i].finish(lambda h: res.at[pl.ds(h * half, half)])
+        src = res if i in (SUM_A, SUM_B) else res.at[rows((1 - yh) * 32, 32)]
+        tails[i] = remote(src, ybuf, ysem, (), yother)
 
     loads[14].wait()
     loads[15].wait()
@@ -783,8 +789,6 @@
         out_ref[j] = dot(dx_ref[:, cols], mixed_ref[...], (0, 0)).reshape(4, 64, 256)
         return carry
 
-    lax.fori_loop(0, 4, out_tile, 0)
-    first[OUT].start()
     sums[...] = jnp.zeros_like(sums)
 
     def block(b, carry):
@@ -807,25 +811,22 @@
         sums[...] += dot(match_ref[at, :], d_qkv, (0, 0))
         return carry
 
-    lax.fori_loop(0, 4, block, 0)
+    def pair(b, carry):
+        return block(2 * b + 1, block(2 * b, carry))
+
+    lax.fori_loop(0, 2, pair, 0)
     for i in (UP_A, UP_B):
         second[i].middle()
     for i in (DOWN_A, DOWN_B):
         first[i].middle()
-    lax.fori_loop(4, 8, block, 0)
+    lax.fori_loop(2, 4, pair, 0)
+    sums4[...] = sums[...].reshape(4, 4, 16, 768)
+    first[SUM_A].start()
+    first[SUM_B].start()
+    lax.fori_loop(0, 4, out_tile, 0)
+    first[OUT].start()
     high, low = halves(sums[...])
 
-    def grad_tile(j, carry):
-        cols = rows(j * 256, 256)
-        table = ht_ref[:, cols]
-        total = dot(table, high, (0, 0)) + dot(table, low, (0, 0))
-        qk_ref[j] = total[:, :512].reshape(4, 64, 512)
-        v_ref[j] = total[:, 512:].reshape(4, 64, 256)
-        return carry
-
-    lax.fori_loop(0, 4, grad_tile, 0)
-    first[QK].start()
-    first[VALUE].start()
     dt_ref[...] = jnp.zeros_like(dt_ref)
     for n, w in enumerate((wq_ref, wk_ref, wv_ref)):
         cols = slice(n * 256, (n + 1) * 256)
@@ -848,25 +849,40 @@
     small4[...] = small.reshape(4, 4, 64, 128)
     first[SMALL].start()
 
-    first[OUT].middle()
+    first[SUM_A].middle()
+    first[SUM_B].middle()
     send_tail(UP_A)
     send_tail(UP_B)
     turn(DOWN_A)
     turn(DOWN_B)
-    for i in (QK, VALUE, SMALL):
-        first[i].middle()
-    turn(OUT)
+    turn(SUM_A)
+    turn(SUM_B)
+    first[OUT].middle()
+    first[SMALL].middle()
+    second[SUM_A].middle()
+    second[SUM_B].middle()
     second[DOWN_A].middle()
     second[DOWN_B].middle()
-    for i in (QK, VALUE, SMALL):
-        turn(i)
+    send_tail(SUM_A)
+    send_tail(SUM_B)
+    turn(OUT)
+    turn(SMALL)
+    for i in (SUM_A, SUM_B):
+        tails[i].wait_recv()
+    full_a[x, z] = ends[SUM_A][0][...] + ends[SUM_A][1][...]
+    full_b[x, z] = ends[SUM_B][0][...] + ends[SUM_B][1][...]
+    near = [remote(full_a.at[x, z], full_a.at[x, z], near_sem, (0, j - 1), at_z(j)) for j in (1, 2, 3)]
+    near += [remote(full_b.at[x, z], full_b.at[x, z], near_sem, (1, j - 1), at_x(j)) for j in (1, 2, 3)]
     send_tail(DOWN_A)
     send_tail(DOWN_B)
     second[OUT].middle()
-    for i in (QK, VALUE, SMALL):
-        second[i].middle()
-    for i in (OUT, SMALL, QK, VALUE):
-        send_tail(i)
+    second[SMALL].middle()
+    for cp in near:
+        cp.wait_recv()
+    wide = [remote(full_a.at[x], full_a.at[x], far_sem, (0, j - 1), at_x(j)) for j in (1, 2, 3)]
+    wide += [remote(full_b.at[:, z], full_b.at[:, z], far_sem, (1, j - 1), at_z(j)) for j in (1, 2, 3)]
+    send_tail(OUT)
+    send_tail(SMALL)
 
     def total(i, put):
         res, ybuf, _ = ends[i]
@@ -882,17 +898,24 @@
         mp_buf[m, pl.ds(k, 8), :] = value
 
     shares = []
-    for i in (UP_A, UP_B, DOWN_A, DOWN_B, OUT, SMALL, QK, VALUE):
+    for i in (UP_A, UP_B, DOWN_A, DOWN_B, SMALL, OUT):
         tails[i].wait_recv()
         if i == SMALL:
             total(i, to_mp)
             shares = [remote(mp_buf.at[m], mp_buf.at[m], mp_sem, (j,), dev) for j, dev in enumerate(peers)]
         else:
             total(i, to_out(outs[i]))
+    for cp in wide:
+        cp.wait_recv()
+    table = ht_ref[:, rows((d // 4) * 128, 128)]
+    for n, ref in enumerate((full_a, full_b)):
+        high, low = halves(ref[...].reshape(256, 384))
+        mine_ref[:, n * 384 : (n + 1) * 384] = dot(table, high, (0, 0)) + dot(table, low, (0, 0))
+    outs[6][...] = mine_ref[rows((d % 4) * 32, 32), :]
     for cp in shares:
         cp.wait_recv()
     outs[SMALL][...] = mp_buf[0] + mp_buf[1] + mp_buf[2] + mp_buf[3]
-    for cp in [*shares, *tails.values()]:
+    for cp in [*shares, *tails.values(), *near, *wide]:
         cp.wait_send()
     for ring in [*first.values(), *second]:
         ring.drain()
@@ -902,20 +925,19 @@
     vm, dma = pltpu.VMEM, pltpu.SemaphoreType.DMA
     scratch = [vm(shape, kind) for shape, kind in LOADS]
     scratch += [
-        dma((len(LOADS),)), vm((4, 4, 64, 512), F32), vm((4, 4, 64, 256), F32), vm((4, 4, 64, 256), F32),
-        vm((256, 768), F32), vm((256, 1024), F32), vm((32, 1024), F32), vm((4, 32, 128), F32), dma((2, 3)),
+        dma((len(LOADS),)), vm((4, 4, 64, 256), F32), vm((256, 768), F32), vm((4, 4, 16, 768), F32),
+        vm((4, 4, 16, 384), F32), vm((4, 4, 16, 384), F32), dma((2, 2, 3)), dma((2, 2, 3)), vm((128, 768), F32),
+        vm((256, 1024), F32), vm((32, 1024), F32), vm((4, 4, 64, 128), F32), vm((4, 32, 128), F32), dma((2, 3)),
     ]
     for i in range(2, 8):
-        scratch += one_scratch(WIDTH[i]) + [vm((4, 64, WIDTH[i]), F32)]
-        if i == SMALL:
-            scratch += [vm((4, 4, 64, 128), F32)]
+        scratch += one_scratch(WIDTH[i], PART[i]) + [vm((4, PART[i], WIDTH[i]), F32)]
     for i in range(8):
-        scratch += two_scratch(WIDTH[i])
+        scratch += two_scratch(WIDTH[i], PART[i], 16 if i in (SUM_A, SUM_B) else 32)
     return pl.pallas_call(
         tail_kernel,
-        out_shape=tuple(jax.ShapeDtypeStruct((32, w), F32) for w in WIDTH),
+        out_shape=tuple(jax.ShapeDtypeStruct((32, w), F32) for w in (*WIDTH[:6], 768)),
         in_specs=[ANY] * len(LOADS),
-        out_specs=tuple([VMEM] * 8),
+        out_specs=tuple([VMEM] * 7),
         scratch_shapes=scratch,
         compiler_params=params(2),
         name="tail",
@@ -923,12 +945,12 @@
 
 
 def write_kernel(
-    up_a, up_b, down_a, down_b, out_ref, qk_ref, value_ref, small_ref,
+    up_a, up_b, down_a, down_b, out_ref, small_ref, qkv_ref,
     o_q, o_k, o_v, o_out, o_up, o_down, o_actor, o_critic, o_final, o_mlp, o_attn,
 ):
-    o_q[...] = qk_ref[:, :256]
-    o_k[...] = qk_ref[:, 256:]
-    o_v[...] = value_ref[...]
+    o_q[...] = qkv_ref[:, :256]
+    o_k[...] = qkv_ref[:, 256:512]
+    o_v[...] = qkv_ref[:, 512:]
     o_up[:, :512] = up_a[...]
     o_up[:, 512:] = up_b[...]
     o_out[...] = out_ref[...]
@@ -949,7 +971,7 @@
     return pl.pallas_call(
         write_kernel,
         out_shape=tuple(sd(shape, F32) for shape in shapes),
-        in_specs=[VMEM] * 8,
+        in_specs=[VMEM] * 7,
         out_specs=tuple([VMEM] * 11),
         name="write_outputs",
     )(*parts)

time: 184 us -> 177 us (0.962)
  Pallas kernels: 181 us -> 174 us
    pallas_call x1, Pallas kernels: 65.5 us -> 59.6 us  [tail(): pl.pallas_call(tail_kernel, out_shape=tuple((jax.ShapeDtypeStruct((32, w)...]
where the time goes in v3:
time: 177 us; the launch traced here: 176 us
  Pallas kernels  174 us (98%)
    pallas_call x1, Pallas kernels, policy(): pl.pallas_call(functools.partial(policy_kernel, token_total), out_shape=(...  112 us
    pallas_call x1, Pallas kernels, tail(): pl.pallas_call(tail_kernel, out_shape=tuple((jax.ShapeDtypeStruct((32, w)...  59.6 us

profile of v3, /device:TPU:0, one launch (start us, length us, event | category | flops | bytes accessed | tf_op | source)
XLA Modules:
  0.0 175.7 jit_solution(9466864822690584012)
XLA Ops:
  0.6 1.3 reshape.57.critic_ref
  1.9 112.2 %policy.1 = (bf16[1024,768]{1,0:T(8,128)(2,1)}, bf16[1024,256]{1,0:T(8,128)(2,1)}, bf16[1024,256]{1,0:T(8,128)(2,1)}, bf16[256,1024]{1,0:T(8,128)(2,1)}, f32[4,4...) custom-call(s32[1,64]{1,0:T(1,128)} %bitcast.23, ...), custom_call_target="tpu_custom_call" | custom-call | tf_op jit(solution)/shard_map/policy/pallas_call | solution.py:689
  114.1 59.6 %tail.1 = (f32[32,512]{1,0:T(8,128)}, f32[32,512]{1,0:T(8,128)}, f32[32,512]{1,0:T(8,128)}, f32[32,512]{1,0:T(8,128)}, f32[32,256]{1,0:T(8,128)}, /*index=5*/f32[32,128]{1,0:T(8,128)}, f32[32,768]{1,0:T(8,128)}) custom-call(f32[4,4,64,1024]{3,2,1,0:T(8,128)} %get-tuple-element.40.refs_0_, bf16[1024,1024]{1,0:T(8,128)(2,1)} %get-tuple-element.41.refs_1_, ...), custom_call_target="tpu_custom_call" | custom-call | tf_op jit(solution)/shard_map/tail/pallas_call | solution.py:936
  173.8 1.8 %write_outputs.1 = (f32[32,256]{1,0:T(8,128)}, f32[32,256]{1,0:T(8,128)}, f32[32,256]{1,0:T(8,128)}, f32[32,256]{1,0:T(8,128)}, f32[32,1024]{1,0:T(8,128)}, /*in...) custom-call(f32[32,512]{1,0:T(8,128)} %get-tuple-element.51.up_a, ...), custom_call_target="tpu_custom_call" | custom-call | tf_op jit(solution)/shard_map/write_outputs/pallas_call | solution.py:971

commit v4 on v3

--- a/solution.py
+++ b/solution.py
@@ -396,8 +396,8 @@
     token_total,
     init_ref, act_ref, scale_ref, next_ref, rew_ref, obs_ref, gain_attn, wq_ref, wk_ref, wv_ref, wo_ref,
     gain_mlp, gain_fin, actor_ref, critic_ref, up_hbm, down_hbm,
-    qkv_out, match_out, mixed_out, ht_out, down_out, low_one, gh_ref, g_fin, g_mlp, res_a, res_b,
-    qkv_ref, match_ref, mixed_ref, ht_ref, flush_sem,
+    ht_out, down_out, gh_ref, g_fin, g_mlp, res_a, res_b, state_sums, out_ref,
+    low_one, qkv_ref, match_ref, mixed_ref, ht_ref, flush_sem,
     r_init, r_act, r_scale, roll_sem, tables, st_ref, own_ref, head_f, heads,
     w_up, w_down, w_sem,
     p, near_own, near_far, far, whole, h_two, up_rows, hidden, low_two, d_up, x_one, dx_two, buf_a, buf_b,
@@ -499,9 +499,6 @@
     attend(1 - c, l)
     sums.give_own()
     attend(c, l)
-    flush(qkv_ref, qkv_out)
-    flush(match_ref, match_out)
-    flush(mixed_ref, mixed_out)
     for h in range(2):
         at = pl.ds(h * 128, 128)
         mine = match_ref[rows(block_at(h, c, l), 128), :]
@@ -651,6 +648,30 @@
     flush(grad_down, down_out)
     gather.drain()
 
+    def attend_back(core, low):
+        lax.fori_loop(0, 2, functools.partial(back_block, core, low), 0, unroll=True)
+
+    def back_block(core, low, h, carry):
+        at = rows(block_at(h, core, low), 128)
+        d_mixed = dot(low_one[at, :], wo_ref[...], (1, 1)).astype(BF16)
+        qkv = qkv_ref[at, :]
+        parts = [[], [], []]
+        for n in range(2):
+            q, k, v = (qkv[:, j * 256 + n * 128 : j * 256 + (n + 1) * 128] for j in range(3))
+            up = d_mixed[:, n * 128 : (n + 1) * 128]
+            probs = block_probs(q, k)
+            d_probs = dot(up, v, (1, 1))
+            parts[2].append(dot(probs.astype(BF16), up, (0, 0)).astype(BF16))
+            d_scores = (
+                probs * (d_probs - jnp.sum(probs * d_probs, axis=-1, keepdims=True)) * SCALE
+            ).astype(BF16)
+            parts[0].append(dot(d_scores, k, (1, 0)).astype(BF16))
+            parts[1].append(dot(d_scores, q, (0, 0)).astype(BF16))
+        d_qkv = jnp.concatenate([*parts[0], *parts[1], *parts[2]], axis=1)
+        state_sums[...] += dot(match_ref[at, :], d_qkv, (0, 0))
+        return carry
+
+    state_sums[...] = jnp.zeros_like(state_sums)
     gather = Gather(buf_b, whole, low_one, gs_e)
     for h, k in CHUNKS:
         sums.take(h, k)
@@ -665,17 +686,28 @@
         by_blocks(64, 32, body)
         gather.send(h, k)
     sums.drain()
+    attend_back(c, l)
     for h, k in CHUNKS:
         gather.take_core(h, k)
     for h in range(2):
         gather.take_far(h, 0)
     for ring in rings:
         ring.middle()
+    attend_back(1 - c, l)
     for h in range(2):
         gather.take_far(h, 1)
+    attend_back(c, 1 - l)
     for h, k in CHUNKS:
         gather.take_fwd(h, k)
     gather.drain()
+    attend_back(1 - c, 1 - l)
+
+    def out_tile(j, carry):
+        cols = rows(j * 256, 256)
+        out_ref[j] = dot(low_one[:, cols], mixed_ref[...], (0, 0)).reshape(4, 64, 256)
+        return carry
+
+    lax.fori_loop(0, 4, out_tile, 0)
     for ring, res in zip(rings, (res_a, res_b)):
         ring.finish(lambda h, res=res: res.at[pl.ds(h * 2, 2)])
     for ring in rings:
@@ -689,15 +721,15 @@
     return pl.pallas_call(
         functools.partial(policy_kernel, token_total),
         out_shape=(
-            sd((1024, 768), BF16), sd((1024, 256), BF16), sd((1024, 256), BF16), sd((256, 1024), BF16),
-            sd((4, 4, 64, 1024), F32), sd((1024, 1024), BF16), sd((1024, 128), F32), sd((8, 1024), F32),
-            sd((8, 1024), F32), sd((4, 64, 512), F32), sd((4, 64, 512), F32),
+            sd((256, 1024), BF16), sd((4, 4, 64, 1024), F32), sd((1024, 128), F32), sd((8, 1024), F32),
+            sd((8, 1024), F32), sd((4, 64, 512), F32), sd((4, 64, 512), F32), sd((256, 768), F32),
+            sd((4, 4, 64, 256), F32),
         ),
         in_specs=[VMEM] * 15 + [ANY] * 2,
-        out_specs=tuple([ANY] * 5 + [VMEM] * 6),
+        out_specs=tuple([ANY] * 2 + [VMEM] * 7),
         scratch_shapes=[
-            vm((1024, 768), BF16), vm((1024, 256), BF16), vm((1024, 256), BF16), vm((256, 1024), BF16),
-            pltpu.SemaphoreType.DMA((5,)),
+            vm((1024, 1024), BF16), vm((1024, 768), BF16), vm((1024, 256), BF16), vm((1024, 256), BF16), vm((256, 1024), BF16),
+            pltpu.SemaphoreType.DMA((2,)),
             vm((1, 64), jnp.int32), vm((16, 64), jnp.int32), vm((1, 64), F32), pltpu.SemaphoreType.DMA((2, 3)),
             vm((256, 768), BF16), vm((16, 64), F32), vm((256, 128), F32), vm((32, 1024), F32), vm((128, 1024), BF16),
             vm((1024, 1024), BF16), vm((1024, 1024), BF16), pltpu.SemaphoreType.DMA((2,)),
@@ -723,22 +755,22 @@
 ORDER = ("xz", "zx", "xz", "zx", "zx", "xz", "xz", "zx")
 WIDTH = (512, 512, 512, 512, 256, 128, 384, 384)
 PART = (64, 64, 64, 64, 64, 64, 16, 16)
-LOADS = ((4, 4, 64, 1024), F32), ((1024, 1024), BF16), ((1024, 256), BF16), ((256, 1024), BF16), \
-    ((1024, 768), BF16), ((1024, 256), BF16), ((256, 1024), BF16), ((256, 1024), BF16), \
-    ((1024, 256), BF16), ((1024, 256), BF16), ((1024, 256), BF16), ((1024, 128), F32), \
-    ((8, 1024), F32), ((8, 1024), F32), ((4, 64, 512), F32), ((4, 64, 512), F32)
+LOADS = (
+    ((4, 4, 16, 768), F32), ((4, 64, 512), F32), ((4, 64, 512), F32), ((4, 4, 64, 1024), F32),
+    ((1024, 256), BF16), ((1024, 256), BF16), ((1024, 256), BF16), ((256, 1024), BF16), ((256, 1024), BF16),
+    ((1024, 128), F32), ((8, 1024), F32), ((8, 1024), F32), ((4, 4, 64, 256), F32),
+)
 
 
 def tail_kernel(*refs):
     n = len(LOADS)
     hbm, outs, held, rest = refs[:n], refs[n : n + 7], refs[n + 7 : 2 * n + 7], refs[2 * n + 7 :]
-    load_sem, out_ref, sums, sums4, full_a, full_b, near_sem, far_sem, mine_ref, dt_ref, vec_ref, small4, mp_buf, mp_sem = rest[:14]
-    rest = rest[14:]
-    down_ref, dx_ref, mixed_ref, wo_ref, qkv_ref, match_ref, ht_ref, obs_ref = held[:8]
-    wq_ref, wk_ref, wv_ref, small_ref, gf_ref, gm_ref, res_a, res_b = held[8:]
+    load_sem, full_a, full_b, near_sem, far_sem, mine_ref, dt_ref, vec_ref, small4, mp_buf, mp_sem = rest[:11]
+    rest = rest[11:]
+    sums4, res_a, res_b, down_ref, wq_ref, wk_ref, wv_ref, ht_ref, obs_ref, small_ref, gf_ref, gm_ref, out_ref = held
     loads = [pltpu.make_async_copy(a, b, load_sem.at[k]) for k, (a, b) in enumerate(zip(hbm, held))]
-    for k in (14, 15, 0, *range(1, 14)):
-        loads[k].start()
+    for cp in loads:
+        cp.start()
     d, m, c, l = place()
     x, z, yh = axes_place()
     yother = (d + 1 - 2 * yh, m)
@@ -774,59 +806,19 @@
         src = res if i in (SUM_A, SUM_B) else res.at[rows((1 - yh) * 32, 32)]
         tails[i] = remote(src, ybuf, ysem, (), yother)
 
-    loads[14].wait()
-    loads[15].wait()
+    loads[0].wait()
+    first[SUM_A].start()
+    first[SUM_B].start()
+    loads[1].wait()
+    loads[2].wait()
     second[UP_A].start()
     second[UP_B].start()
-    loads[0].wait()
+    loads[3].wait()
     first[DOWN_A].start()
     first[DOWN_B].start()
-    for k in range(1, 14):
-        loads[k].wait()
-
-    def out_tile(j, carry):
-        cols = rows(j * 256, 256)
-        out_ref[j] = dot(dx_ref[:, cols], mixed_ref[...], (0, 0)).reshape(4, 64, 256)
-        return carry
-
-    sums[...] = jnp.zeros_like(sums)
-
-    def block(b, carry):
-        at = rows(b * 128, 128)
-        d_mixed = dot(dx_ref[at, :], wo_ref[...], (1, 1)).astype(BF16)
-        qkv = qkv_ref[at, :]
-        parts = [[], [], []]
-        for h in range(2):
-            q, k, v = (qkv[:, n * 256 + h * 128 : n * 256 + (h + 1) * 128] for n in range(3))
-            up = d_mixed[:, h * 128 : (h + 1) * 128]
-            probs = block_probs(q, k)
-            d_probs = dot(up, v, (1, 1))
-            parts[2].append(dot(probs.astype(BF16), up, (0, 0)).astype(BF16))
-            d_scores = (
-                probs * (d_probs - jnp.sum(probs * d_probs, axis=-1, keepdims=True)) * SCALE
-            ).astype(BF16)
-            parts[0].append(dot(d_scores, k, (1, 0)).astype(BF16))
-            parts[1].append(dot(d_scores, q, (0, 0)).astype(BF16))
-        d_qkv = jnp.concatenate([*parts[0], *parts[1], *parts[2]], axis=1)
-        sums[...] += dot(match_ref[at, :], d_qkv, (0, 0))
-        return carry
-
-    def pair(b, carry):
-        return block(2 * b + 1, block(2 * b, carry))
-
-    lax.fori_loop(0, 2, pair, 0)
-    for i in (UP_A, UP_B):
-        second[i].middle()
-    for i in (DOWN_A, DOWN_B):
-        first[i].middle()
-    lax.fori_loop(2, 4, pair, 0)
-    sums4[...] = sums[...].reshape(4, 4, 16, 768)
-    first[SUM_A].start()
-    first[SUM_B].start()
-    lax.fori_loop(0, 4, out_tile, 0)
-    first[OUT].start()
-    high, low = halves(sums[...])
-
+    for cp in loads[4:]:
+        cp.wait()
+    high, low = halves(sums4[...].reshape(256, 768))
     dt_ref[...] = jnp.zeros_like(dt_ref)
     for n, w in enumerate((wq_ref, wk_ref, wv_ref)):
         cols = slice(n * 256, (n + 1) * 256)
@@ -847,42 +839,38 @@
     lowest = (vec - high.astype(F32) - low.astype(F32)).astype(BF16)
     small = small_ref[...] + sum(dot(part, place_at, (0, 0)) for part in (high, low, lowest))
     small4[...] = small.reshape(4, 4, 64, 128)
+    for i in (SUM_A, SUM_B):
+        first[i].middle()
+    first[OUT].start()
     first[SMALL].start()
-
-    first[SUM_A].middle()
-    first[SUM_B].middle()
-    send_tail(UP_A)
-    send_tail(UP_B)
-    turn(DOWN_A)
-    turn(DOWN_B)
-    turn(SUM_A)
-    turn(SUM_B)
-    first[OUT].middle()
-    first[SMALL].middle()
-    second[SUM_A].middle()
-    second[SUM_B].middle()
-    second[DOWN_A].middle()
-    second[DOWN_B].middle()
-    send_tail(SUM_A)
-    send_tail(SUM_B)
-    turn(OUT)
-    turn(SMALL)
+    for i in (SUM_A, SUM_B):
+        turn(i)
+    for i in (UP_A, UP_B, SUM_A, SUM_B):
+        second[i].middle()
+    for i in (DOWN_A, DOWN_B):
+        first[i].middle()
+    for i in (SUM_A, SUM_B, UP_A, UP_B):
+        send_tail(i)
     for i in (SUM_A, SUM_B):
         tails[i].wait_recv()
     full_a[x, z] = ends[SUM_A][0][...] + ends[SUM_A][1][...]
     full_b[x, z] = ends[SUM_B][0][...] + ends[SUM_B][1][...]
     near = [remote(full_a.at[x, z], full_a.at[x, z], near_sem, (0, j - 1), at_z(j)) for j in (1, 2, 3)]
     near += [remote(full_b.at[x, z], full_b.at[x, z], near_sem, (1, j - 1), at_x(j)) for j in (1, 2, 3)]
-    send_tail(DOWN_A)
-    send_tail(DOWN_B)
-    second[OUT].middle()
-    second[SMALL].middle()
+    for i in (OUT, SMALL):
+        first[i].middle()
+    turn(DOWN_A)
+    turn(DOWN_B)
     for cp in near:
         cp.wait_recv()
     wide = [remote(full_a.at[x], full_a.at[x], far_sem, (0, j - 1), at_x(j)) for j in (1, 2, 3)]
     wide += [remote(full_b.at[:, z], full_b.at[:, z], far_sem, (1, j - 1), at_z(j)) for j in (1, 2, 3)]
-    send_tail(OUT)
-    send_tail(SMALL)
+    turn(SMALL)
+    turn(OUT)
+    for i in (DOWN_A, DOWN_B, SMALL, OUT):
+        second[i].middle()
+    for i in (DOWN_A, DOWN_B, SMALL, OUT):
+        send_tail(i)
 
     def total(i, put):
         res, ybuf, _ = ends[i]
@@ -925,8 +913,7 @@
     vm, dma = pltpu.VMEM, pltpu.SemaphoreType.DMA
     scratch = [vm(shape, kind) for shape, kind in LOADS]
     scratch += [
-        dma((len(LOADS),)), vm((4, 4, 64, 256), F32), vm((256, 768), F32), vm((4, 4, 16, 768), F32),
-        vm((4, 4, 16, 384), F32), vm((4, 4, 16, 384), F32), dma((2, 2, 3)), dma((2, 2, 3)), vm((128, 768), F32),
+        dma((len(LOADS),)), vm((4, 4, 16, 384), F32), vm((4, 4, 16, 384), F32), dma((2, 2, 3)), dma((2, 2, 3)), vm((128, 768), F32),
         vm((256, 1024), F32), vm((32, 1024), F32), vm((4, 4, 64, 128), F32), vm((4, 32, 128), F32), dma((2, 3)),
     ]
     for i in range(2, 8):
@@ -1001,15 +988,15 @@
     def line(vector):
         return vector.reshape(1, -1)
 
-    qkv, match, mixed, h_table, grad_down, dx_one_low, grad_heads, final_terms, mlp_terms, res_a, res_b = policy(
+    h_table, grad_down, grad_heads, final_terms, mlp_terms, res_a, res_b, state_sums, grad_out = policy(
         token_total,
         line(initial_state), actions.T, line(reward_scale), next_state.T, reward_table.T, observe_table,
         line(gain_attn), w_query, w_key, w_value, w_out, line(gain_mlp), line(gain_final),
         actor_head.T, line(critic_head), w_up, w_down,
     )
     parts = tail(
-        grad_down, dx_one_low, mixed, w_out, qkv, match, h_table, observe_table, w_query, w_key, w_value,
-        grad_heads, final_terms, mlp_terms, res_a, res_b,
+        state_sums.reshape(4, 4, 16, 768), res_a, res_b, grad_down, w_query, w_key, w_value, h_table,
+        observe_table, grad_heads, final_terms, mlp_terms, grad_out,
     )
     q, k, v, out, up, down, actor, critic, final, mlp, attn = write_outputs(*parts)
     return (

time: 177 us -> 180 us (1.017)
  Pallas kernels: 174 us -> 177 us
    pallas_call x1, Pallas kernels: 112 us -> 116 us  [policy(): pl.pallas_call(functools.partial(policy_kernel, token_total), out_shape=(...]
where the time goes in v4:
time: 180 us; the launch traced here: 179 us
  Pallas kernels  177 us (98%)
    pallas_call x1, Pallas kernels, policy(): pl.pallas_call(functools.partial(policy_kernel, token_total), out_shape=(...  116 us
    pallas_call x1, Pallas kernels, tail(): pl.pallas_call(tail_kernel, out_shape=tuple((jax.ShapeDtypeStruct((32, w)...  59.1 us

profile of v4, /device:TPU:0, one launch (start us, length us, event | category | flops | bytes accessed | tf_op | source)
XLA Modules:
  0.0 179.1 jit_solution(15050015913004000995)
XLA Ops:
  0.6 1.3 reshape.60.critic_ref
  1.9 116.1 %policy.1 = (bf16[256,1024]{1,0:T(8,128)(2,1)}, f32[4,4,64,1024]{3,2,1,0:T(8,128)}, f32[1024,128]{1,0:T(8,128)}, f32[8,1024]{1,0:T(8,128)}, f32[8,1024]{1,0:T(8,...) custom-call(s32[1,64]{1,0:T(1,128)} %bitcast.25, ...), custom_call_target="tpu_custom_call" | custom-call | tf_op jit(solution)/shard_map/policy/pallas_call | solution.py:721
  118.0 59.1 %tail.1 = (f32[32,512]{1,0:T(8,128)}, f32[32,512]{1,0:T(8,128)}, f32[32,512]{1,0:T(8,128)}, f32[32,512]{1,0:T(8,128)}, f32[32,256]{1,0:T(8,128)}, /*index=5*/f32[32,128]{1,0:T(8,128)}, f32[32,768]{1,0:T(8,128)}) custom-call(f32[4,4,16,768]{3,2,1,0:T(8,128)} %bitcast.17, f32[4,64,512]{2,1,0:T(8,128)} %get-tuple-element.39.refs_1_, ...), custom_call_target="tpu_custom_call" | custom-call | tf_op jit(solution)/shard_map/tail/pallas_call | solution.py:923
  177.1 1.8 %write_outputs.1 = (f32[32,256]{1,0:T(8,128)}, f32[32,256]{1,0:T(8,128)}, f32[32,256]{1,0:T(8,128)}, f32[32,256]{1,0:T(8,128)}, f32[32,1024]{1,0:T(8,128)}, /*in...) custom-call(f32[32,512]{1,0:T(8,128)} %get-tuple-element.47.up_a, ...), custom_call_target="tpu_custom_call" | custom-call | tf_op jit(solution)/shard_map/write_outputs/pallas_call | solution.py:958

commit v5 on v4

--- a/solution.py
+++ b/solution.py
@@ -648,13 +648,9 @@
     flush(grad_down, down_out)
     gather.drain()
 
-    def attend_back(core, low):
-        lax.fori_loop(0, 2, functools.partial(back_block, core, low), 0, unroll=True)
-
-    def back_block(core, low, h, carry):
-        at = rows(block_at(h, core, low), 128)
-        d_mixed = dot(low_one[at, :], wo_ref[...], (1, 1)).astype(BF16)
-        qkv = qkv_ref[at, :]
+    def attend_back(spans):
+        d_mixed = dot(spans_of(low_one, spans), wo_ref[...], (1, 1)).astype(BF16)
+        qkv = spans_of(qkv_ref, spans)
         parts = [[], [], []]
         for n in range(2):
             q, k, v = (qkv[:, j * 256 + n * 128 : j * 256 + (n + 1) * 128] for j in range(3))
@@ -668,8 +664,7 @@
             parts[0].append(dot(d_scores, k, (1, 0)).astype(BF16))
             parts[1].append(dot(d_scores, q, (0, 0)).astype(BF16))
         d_qkv = jnp.concatenate([*parts[0], *parts[1], *parts[2]], axis=1)
-        state_sums[...] += dot(match_ref[at, :], d_qkv, (0, 0))
-        return carry
+        state_sums[...] += dot(spans_of(match_ref, spans), d_qkv, (0, 0))
 
     state_sums[...] = jnp.zeros_like(state_sums)
     gather = Gather(buf_b, whole, low_one, gs_e)
@@ -686,21 +681,27 @@
         by_blocks(64, 32, body)
         gather.send(h, k)
     sums.drain()
-    attend_back(c, l)
+    for h in range(2):
+        attend_back([(block_at(h, c, l), 128)])
     for h, k in CHUNKS:
         gather.take_core(h, k)
     for h in range(2):
         gather.take_far(h, 0)
     for ring in rings:
         ring.middle()
-    attend_back(1 - c, l)
+    for h in range(2):
+        attend_back([(block_at(h, 1 - c, l), 128)])
+    for h in range(2):
+        gather.take_fwd(h, 0)
+    attend_back([(block_at(h, c, 1 - l), 64) for h in range(2)])
+    attend_back([(block_at(h, 1 - c, 1 - l), 64) for h in range(2)])
     for h in range(2):
         gather.take_far(h, 1)
-    attend_back(c, 1 - l)
-    for h, k in CHUNKS:
-        gather.take_fwd(h, k)
+    attend_back([(block_at(h, c, 1 - l) + 64, 64) for h in range(2)])
+    for h in range(2):
+        gather.take_fwd(h, 1)
+    attend_back([(block_at(h, 1 - c, 1 - l) + 64, 64) for h in range(2)])
     gather.drain()
-    attend_back(1 - c, 1 - l)
 
     def out_tile(j, carry):
         cols = rows(j * 256, 256)
@@ -841,35 +842,43 @@
     small4[...] = small.reshape(4, 4, 64, 128)
     for i in (SUM_A, SUM_B):
         first[i].middle()
-    first[OUT].start()
-    first[SMALL].start()
-    for i in (SUM_A, SUM_B):
-        turn(i)
-    for i in (UP_A, UP_B, SUM_A, SUM_B):
+    for i in (UP_A, UP_B):
         second[i].middle()
     for i in (DOWN_A, DOWN_B):
         first[i].middle()
-    for i in (SUM_A, SUM_B, UP_A, UP_B):
+    for i in (UP_A, UP_B):
         send_tail(i)
+    for i in (SUM_A, SUM_B):
+        turn(i)
+    first[OUT].start()
+    first[SMALL].start()
+    for i in (DOWN_A, DOWN_B):
+        turn(i)
+    for i in (SUM_A, SUM_B):
+        second[i].middle()
+    for i in (SUM_A, SUM_B):
+        send_tail(i)
+    for i in (DOWN_A, DOWN_B):
+        second[i].middle()
+    for i in (OUT, SMALL):
+        first[i].middle()
     for i in (SUM_A, SUM_B):
         tails[i].wait_recv()
     full_a[x, z] = ends[SUM_A][0][...] + ends[SUM_A][1][...]
     full_b[x, z] = ends[SUM_B][0][...] + ends[SUM_B][1][...]
     near = [remote(full_a.at[x, z], full_a.at[x, z], near_sem, (0, j - 1), at_z(j)) for j in (1, 2, 3)]
     near += [remote(full_b.at[x, z], full_b.at[x, z], near_sem, (1, j - 1), at_x(j)) for j in (1, 2, 3)]
-    for i in (OUT, SMALL):
-        first[i].middle()
-    turn(DOWN_A)
-    turn(DOWN_B)
+    for i in (DOWN_A, DOWN_B):
+        send_tail(i)
     for cp in near:
         cp.wait_recv()
     wide = [remote(full_a.at[x], full_a.at[x], far_sem, (0, j - 1), at_x(j)) for j in (1, 2, 3)]
     wide += [remote(full_b.at[:, z], full_b.at[:, z], far_sem, (1, j - 1), at_z(j)) for j in (1, 2, 3)]
-    turn(SMALL)
-    turn(OUT)
-    for i in (DOWN_A, DOWN_B, SMALL, OUT):
+    for i in (SMALL, OUT):
+        turn(i)
+    for i in (SMALL, OUT):
         second[i].middle()
-    for i in (DOWN_A, DOWN_B, SMALL, OUT):
+    for i in (SMALL, OUT):
         send_tail(i)
 
     def total(i, put):

time: 180 us -> 183 us (1.017)
  Pallas kernels: 177 us -> 180 us
    pallas_call x1, Pallas kernels: 59.1 us -> 64.2 us  [tail(): pl.pallas_call(tail_kernel, out_shape=tuple((jax.ShapeDtypeStruct((32, w)...]
    pallas_call x1, Pallas kernels: 116 us -> 114 us  [policy(): pl.pallas_call(functools.partial(policy_kernel, token_total), out_shape=(...]
where the time goes in v5:
time: 183 us; the launch traced here: 182 us
  Pallas kernels  180 us (98%)
    pallas_call x1, Pallas kernels, policy(): pl.pallas_call(functools.partial(policy_kernel, token_total), out_shape=(...  114 us
    pallas_call x1, Pallas kernels, tail(): pl.pallas_call(tail_kernel, out_shape=tuple((jax.ShapeDtypeStruct((32, w)...  64.2 us

profile of v5, /device:TPU:0, one launch (start us, length us, event | category | flops | bytes accessed | tf_op | source)
XLA Modules:
  0.0 181.9 jit_solution(3657177380854994159)
XLA Ops:
  0.6 1.3 reshape.60.critic_ref
  1.9 113.8 %policy.1 = (bf16[256,1024]{1,0:T(8,128)(2,1)}, f32[4,4,64,1024]{3,2,1,0:T(8,128)}, f32[1024,128]{1,0:T(8,128)}, f32[8,1024]{1,0:T(8,128)}, f32[8,1024]{1,0:T(8,...) custom-call(s32[1,64]{1,0:T(1,128)} %bitcast.25, ...), custom_call_target="tpu_custom_call" | custom-call | tf_op jit(solution)/shard_map/policy/pallas_call | solution.py:722
  115.7 64.2 %tail.1 = (f32[32,512]{1,0:T(8,128)}, f32[32,512]{1,0:T(8,128)}, f32[32,512]{1,0:T(8,128)}, f32[32,512]{1,0:T(8,128)}, f32[32,256]{1,0:T(8,128)}, /*index=5*/f32[32,128]{1,0:T(8,128)}, f32[32,768]{1,0:T(8,128)}) custom-call(f32[4,4,16,768]{3,2,1,0:T(8,128)} %bitcast.17, f32[4,64,512]{2,1,0:T(8,128)} %get-tuple-element.39.refs_1_, ...), custom_call_target="tpu_custom_call" | custom-call | tf_op jit(solution)/shard_map/tail/pallas_call | solution.py:932
  179.9 1.8 %write_outputs.1 = (f32[32,256]{1,0:T(8,128)}, f32[32,256]{1,0:T(8,128)}, f32[32,256]{1,0:T(8,128)}, f32[32,256]{1,0:T(8,128)}, f32[32,1024]{1,0:T(8,128)}, /*in...) custom-call(f32[32,512]{1,0:T(8,128)} %get-tuple-element.47.up_a, ...), custom_call_target="tpu_custom_call" | custom-call | tf_op jit(solution)/shard_map/write_outputs/pallas_call | solution.py:967

commit v6 on v5

--- a/solution.py
+++ b/solution.py
@@ -814,10 +814,7 @@
     loads[2].wait()
     second[UP_A].start()
     second[UP_B].start()
-    loads[3].wait()
-    first[DOWN_A].start()
-    first[DOWN_B].start()
-    for cp in loads[4:]:
+    for cp in loads[3:]:
         cp.wait()
     high, low = halves(sums4[...].reshape(256, 768))
     dt_ref[...] = jnp.zeros_like(dt_ref)
@@ -844,24 +841,24 @@
         first[i].middle()
     for i in (UP_A, UP_B):
         second[i].middle()
-    for i in (DOWN_A, DOWN_B):
-        first[i].middle()
+    for i in (DOWN_A, DOWN_B, OUT, SMALL):
+        first[i].start()
+    for i in (SUM_A, SUM_B):
+        turn(i)
     for i in (UP_A, UP_B):
         send_tail(i)
+    for i in (DOWN_A, DOWN_B, OUT, SMALL):
+        first[i].middle()
     for i in (SUM_A, SUM_B):
-        turn(i)
-    first[OUT].start()
-    first[SMALL].start()
+        second[i].middle()
     for i in (DOWN_A, DOWN_B):
         turn(i)
-    for i in (SUM_A, SUM_B):
-        second[i].middle()
     for i in (SUM_A, SUM_B):
         send_tail(i)
     for i in (DOWN_A, DOWN_B):
         second[i].middle()
-    for i in (OUT, SMALL):
-        first[i].middle()
+    for i in (SMALL, OUT):
+        turn(i)
     for i in (SUM_A, SUM_B):
         tails[i].wait_recv()
     full_a[x, z] = ends[SUM_A][0][...] + ends[SUM_A][1][...]
@@ -874,8 +871,6 @@
         cp.wait_recv()
     wide = [remote(full_a.at[x], full_a.at[x], far_sem, (0, j - 1), at_x(j)) for j in (1, 2, 3)]
     wide += [remote(full_b.at[:, z], full_b.at[:, z], far_sem, (1, j - 1), at_z(j)) for j in (1, 2, 3)]
-    for i in (SMALL, OUT):
-        turn(i)
     for i in (SMALL, OUT):
         second[i].middle()
     for i in (SMALL, OUT):

time: 183 us -> 181 us (0.989)
  Pallas kernels: 180 us -> 178 us
where the time goes in v6:
time: 181 us; the launch traced here: 180 us
  Pallas kernels  178 us (98%)
    pallas_call x1, Pallas kernels, policy(): pl.pallas_call(functools.partial(policy_kernel, token_total), out_shape=(...  114 us
    pallas_call x1, Pallas kernels, tail(): pl.pallas_call(tail_kernel, out_shape=tuple((jax.ShapeDtypeStruct((32, w)...  62.5 us

profile of v6, /device:TPU:0, one launch (start us, length us, event | category | flops | bytes accessed | tf_op | source)
XLA Modules:
  0.0 180.2 jit_solution(2657522301298646040)
XLA Ops:
  0.6 1.3 reshape.60.critic_ref
  1.9 113.8 %policy.1 = (bf16[256,1024]{1,0:T(8,128)(2,1)}, f32[4,4,64,1024]{3,2,1,0:T(8,128)}, f32[1024,128]{1,0:T(8,128)}, f32[8,1024]{1,0:T(8,128)}, f32[8,1024]{1,0:T(8,...) custom-call(s32[1,64]{1,0:T(1,128)} %bitcast.25, ...), custom_call_target="tpu_custom_call" | custom-call | tf_op jit(solution)/shard_map/policy/pallas_call | solution.py:722
  115.7 62.5 %tail.1 = (f32[32,512]{1,0:T(8,128)}, f32[32,512]{1,0:T(8,128)}, f32[32,512]{1,0:T(8,128)}, f32[32,512]{1,0:T(8,128)}, f32[32,256]{1,0:T(8,128)}, /*index=5*/f32[32,128]{1,0:T(8,128)}, f32[32,768]{1,0:T(8,128)}) custom-call(f32[4,4,16,768]{3,2,1,0:T(8,128)} %bitcast.17, f32[4,64,512]{2,1,0:T(8,128)} %get-tuple-element.39.refs_1_, ...), custom_call_target="tpu_custom_call" | custom-call | tf_op jit(solution)/shard_map/tail/pallas_call | solution.py:927
  178.2 1.8 %write_outputs.1 = (f32[32,256]{1,0:T(8,128)}, f32[32,256]{1,0:T(8,128)}, f32[32,256]{1,0:T(8,128)}, f32[32,256]{1,0:T(8,128)}, f32[32,1024]{1,0:T(8,128)}, /*in...) custom-call(f32[32,512]{1,0:T(8,128)} %get-tuple-element.47.up_a, ...), custom_call_target="tpu_custom_call" | custom-call | tf_op jit(solution)/shard_map/write_outputs/pallas_call | solution.py:962
